TPU v7x, 32 devices: a whole 2x2x4 slice. The times are simulated.
32 devices in a mesh: row: 4 (over y, core), col: 8 (over z, x).
Axes of the slice: x: 2, y: 2, z: 4, core: 2. Of those that a mesh axis runs over, the one named last changes fastest.
Arguments:
- start_field: float32 [1, 2, 4096, 8192], P(None, None, 'col', 'row'), may hold values from -6 to 6
- section_field: float32 [1, 2, 4096, 8192], P(None, None, 'col', 'row'), may hold values from -26 to 26
- start_term: float32 [1, 2, 4096, 8192], P(None, None, 'col', 'row'), may hold values from -6 to 6
- first_term: float32 [1, 2, 4096, 8192], P(None, None, 'col', 'row'), may hold values from -6 to 6
- second_term: float32 [1, 2, 4096, 8192], P(None, None, 'col', 'row'), may hold values from -6 to 6
Outputs:
- next_field: float32 [1, 2, 4096, 8192], P(None, None, 'col', 'row')
All inputs are finite; a program needn't handle non-finite values.
Results may differ from a plain program's by a relative error of at most 0.0001.
Values sent between devices are 32-bit elements; how exact they have to be, the bound alone decides.
A program may use at most 256 MiB of HBM per device.

v0:
```python
import math

import jax
import jax.numpy as jnp
from jax import lax
from jax.sharding import PartitionSpec as P

RADIX = 128


viscous_rate = 1.5
wave_scale = 3.0
series_terms = 12


def section_weights(wave_x, wave_y, length):
    square = wave_x * wave_x + wave_y * wave_y
    kappa_x = wave_scale * wave_x.astype(jnp.float32) / length
    kappa_y = wave_scale * wave_y.astype(jnp.float32) / length
    kappa_sq = kappa_x * kappa_x + kappa_y * kappa_y
    zvalue = -viscous_rate * kappa_sq
    damping = jnp.exp(zvalue)
    near_zero = 27 * square < 2 * length * length

    def series(degree):
        running = jnp.full_like(zvalue, 1.0 / math.factorial(series_terms - 1 + degree))
        for term_index in range(series_terms - 2, -1, -1):
            running = running * zvalue + 1.0 / math.factorial(term_index + degree)
        return running

    clamped = jnp.where(near_zero, -1.0, zvalue)
    exp_clamped = jnp.exp(clamped)
    closed_one = (exp_clamped - 1.0) / clamped
    closed_two = (exp_clamped - 1.0 - clamped) / (clamped * clamped)
    closed_three = (exp_clamped - 1.0 - clamped - 0.5 * clamped * clamped) / (
        clamped * clamped * clamped
    )
    phi_one = jnp.where(near_zero, series(1), closed_one)
    phi_two = jnp.where(near_zero, series(2), closed_two)
    phi_three = jnp.where(near_zero, series(3), closed_three)
    weight_a = phi_one - 3.0 * phi_two + 4.0 * phi_three
    weight_b = phi_two - 2.0 * phi_three
    weight_c = 4.0 * phi_three - phi_two
    keep_mask = ((3 * jnp.abs(wave_x) < length) & (3 * jnp.abs(wave_y) < length)).astype(
        jnp.float32
    )
    inverse_sq = length * length / (9.0 * jnp.maximum(square, 1).astype(jnp.float32))
    return (damping, weight_a, weight_b, weight_c, kappa_x, kappa_y, keep_mask, inverse_sq)


def section_table(count_in, count_out, period, direction):
    row_ids = lax.broadcasted_iota(jnp.int32, (count_in, count_out), 0)
    col_ids = lax.broadcasted_iota(jnp.int32, (count_in, count_out), 1)
    angles = direction * 2.0 * math.pi / period * (row_ids * col_ids % period).astype(jnp.float32)
    cosine = jnp.cos(angles)
    sine_part = jnp.sin(angles)
    return jnp.stack(
        [jnp.stack([cosine, sine_part], axis=1), jnp.stack([-sine_part, cosine], axis=1)], axis=0
    )


def twiddle(count_c, count_b, period, direction):
    row_ids = lax.broadcasted_iota(jnp.int32, (count_c, count_b), 0)
    col_ids = lax.broadcasted_iota(jnp.int32, (count_c, count_b), 1)
    angles = direction * 2.0 * math.pi / period * (row_ids * col_ids % period).astype(jnp.float32)
    return (jnp.cos(angles), jnp.sin(angles))


def rotate(values, cosine, sine_part):
    return jnp.stack(
        [values[0] * cosine - values[1] * sine_part, values[0] * sine_part + values[1] * cosine]
    )


def product(equation, left, right):
    return jnp.einsum(equation, left, right, precision=lax.Precision.HIGH)


def lines_inverse(pieces):
    parts, count_k, length = pieces.shape
    count_b = RADIX
    count_a = length // count_b
    shaped = pieces.reshape((parts, count_k, count_a, count_b))
    first = product("pkab,pasc->skcb", shaped, section_table(count_a, count_a, count_a, 1.0))
    first = rotate(first, *twiddle(count_a, count_b, length, 1.0))
    second = product("pkcb,pbsd->skcd", first, section_table(count_b, count_b, count_b, 1.0))
    return second.reshape((parts, count_k, length))


def lines_forward(pieces):
    parts, count_k, length = pieces.shape
    count_d = RADIX
    count_c = length // count_d
    shaped = pieces.reshape((parts, count_k, count_c, count_d))
    first = product("pkcd,pdsf->skcf", shaped, section_table(count_d, count_d, count_d, -1.0))
    first = rotate(first, *twiddle(count_c, count_d, length, -1.0))
    second = product("pkcf,pcse->skef", first, section_table(count_c, count_c, count_c, -1.0))
    return second.reshape((parts, count_k, length))


def turned_table(count_c, count_b, period, direction):
    c_ids = lax.broadcasted_iota(jnp.int32, (count_c, count_b, count_b), 0)
    b_ids = lax.broadcasted_iota(jnp.int32, (count_c, count_b, count_b), 1)
    d_ids = lax.broadcasted_iota(jnp.int32, (count_c, count_b, count_b), 2)
    steps = b_ids * (c_ids + count_c * d_ids) % period
    angles = direction * 2.0 * math.pi / period * steps.astype(jnp.float32)
    return jnp.cos(angles), jnp.sin(angles)


def columns_inverse(pieces, table):
    parts, half_count, count_y = pieces.shape
    count_a = half_count // RADIX
    count_c = 2 * count_a
    shaped = pieces.reshape((parts, count_a, RADIX, count_y))
    first = product("paby,pasc->csby", shaped, section_table(count_a, count_c, count_c, 1.0))
    return product("csby,csbd->cdy", first, table)


def columns_forward(grid, table):
    count_c, count_d, count_y = grid.shape
    half_count = count_c // 2
    first = product("cdy,cpfd->cpfy", grid, table)
    second = product(
        "cpfy,pcse->sefy", first, section_table(count_c, half_count, count_c, -1.0)
    )
    return second.reshape((2, half_count * count_d, count_y))


def to_columns(lines):
    return lax.all_to_all(lines, ("col", "row"), split_axis=2, concat_axis=1, tiled=True)


def to_lines(columns):
    return lax.all_to_all(columns, ("col", "row"), split_axis=1, concat_axis=2, tiled=True)


def positions(shape, start_x, start_y, length):
    wave_x = start_x + lax.broadcasted_iota(jnp.int32, shape, 0)
    index_y = start_y + lax.broadcasted_iota(jnp.int32, shape, 1)
    wave_y = jnp.where(index_y < length // 2, index_y, index_y - length)
    return wave_x, wave_y


def nonlinear(section_field, length):
    block_x = section_field.shape[1]
    lines = lax.all_to_all(section_field, "row", split_axis=1, concat_axis=2, tiled=True)
    count_k = lines.shape[1]
    start_x = lax.axis_index("col") * block_x + lax.axis_index("row") * count_k
    wave_x, wave_y = positions((count_k, length), start_x, 0, length)
    square = wave_x * wave_x + wave_y * wave_y
    kappa_x = wave_scale * wave_x.astype(jnp.float32) / length
    kappa_y = wave_scale * wave_y.astype(jnp.float32) / length
    keep = (3 * jnp.abs(wave_x) < length) & (3 * jnp.abs(wave_y) < length)
    doubled = jnp.where(wave_x == 0, 1.0, 2.0) * (1.0 / length)
    inverse_sq = length * length / (9.0 * jnp.maximum(square, 1).astype(jnp.float32))
    factor = jnp.where(keep, inverse_sq * doubled, 0.0)
    scale_u = kappa_y * factor
    scale_v = kappa_x * factor
    spec_u = jnp.stack([-scale_u * lines[1], scale_u * lines[0]])
    spec_v = jnp.stack([scale_v * lines[1], -scale_v * lines[0]])
    count_c = length // RADIX
    cosine, sine_part = turned_table(count_c, RADIX, length, 1.0)
    table = jnp.stack([cosine, -sine_part], axis=1)
    vel_u = columns_inverse(to_columns(lines_inverse(spec_u)), table)
    vel_v = columns_inverse(to_columns(lines_inverse(spec_v)), table)
    cross = lines_forward(to_lines(columns_forward(vel_u * vel_v, table)))
    square_gap = lines_forward(
        to_lines(columns_forward((vel_v - vel_u) * (vel_v + vel_u), table))
    )
    scale = jnp.where(keep, 1.0 / length, 0.0)
    weight_cross = (kappa_x * kappa_x - kappa_y * kappa_y) * scale
    weight_gap = kappa_x * kappa_y * scale
    term = weight_cross * cross + weight_gap * square_gap
    return lax.all_to_all(term, "row", split_axis=2, concat_axis=1, tiled=True)


def per_device(start_field, section_field, start_term, first_term, second_term):
    members = start_field.shape[0]
    block_x = start_field.shape[2]
    block_y = start_field.shape[3]
    length = block_y * lax.axis_size("row")
    wave_x, wave_y = positions(
        (block_x, block_y),
        lax.axis_index("col") * block_x,
        lax.axis_index("row") * block_y,
        length,
    )
    damping, weight_a, weight_b, weight_c = section_weights(wave_x, wave_y, length)[:4]
    linear = (
        damping * start_field
        + weight_a * start_term
        + 2.0 * weight_b * (first_term + second_term)
    )
    linear, weight_c = lax.optimization_barrier((linear, weight_c))
    section_term = jnp.stack([nonlinear(section_field[m], length) for m in range(members)])
    return linear + weight_c * section_term


def solution(mesh):
    return jax.shard_map(
        per_device,
        mesh=mesh,
        in_specs=(
            P(None, None, "col", "row"),
            P(None, None, "col", "row"),
            P(None, None, "col", "row"),
            P(None, None, "col", "row"),
            P(None, None, "col", "row"),
        ),
        out_specs=P(None, None, "col", "row"),
        check_vma=False,
    )
```

profile of v0, /device:TPU:9, one launch (start us, length us, event | category | flops | bytes accessed | tf_op | source)
XLA Modules:
  0.0 1389.5 jit_solution(14746386528013879035)
XLA Ops:
  0.0 15.4 %copy.229 = f32[1,2,512,2048]{3,1,2,0:T(2,128)} copy(f32[1,2,512,2048]{3,2,1,0:T(8,128)} %param.6) | data formatting | bytes 16777216 | tf_op args[1]
  23.8 90.1 %all-to-all-done = f32[2,512,2048]{2,0,1:T(2,128)} async-done(((f32[2,512,2048]{2,0,1:T(2,128)}), f32[2,512,2048]{2,0,1:T(2,128)}, u32[]{:S(2)}, u32[]{:S(2)}) %all-to-all-start) | async-done | bytes 8388640 | tf_op jit(solution)/shard_map/all_to_all | solution.py:146
  182.1 31.3 %copy.115 = f32[2,128,8192]{1,0,2:T(2,128)} copy(f32[2,128,8192]{1,2,0:T(8,128)S(1)} %bitcast.248) | data formatting | bytes 16777216 | tf_op jit(solution)/shard_map/reshape | solution.py:87
  232.1 31.7 %copy.119 = f32[2,128,8192]{1,0,2:T(2,128)} copy(f32[2,128,8192]{1,2,0:T(8,128)S(1)} %bitcast.247) | data formatting | bytes 16777216 | tf_op jit(solution)/shard_map/reshape | solution.py:87
  263.7 136.4 %all-to-all-done.1 = f32[2,128,8192]{1,0,2:T(2,128)} async-done(((f32[2,128,8192]{1,0,2:T(2,128)}), f32[2,128,8192]{1,0,2:T(2,128)}, u32[]{:S(2)}, u32[]{:S(2)}) %all-to-all-start.1) | async-done | bytes 8388640 | tf_op jit(solution)/shard_map/all_to_all | solution.py:130
  412.5 19.0 %fusion.171 = (f32[64,1,128,128]{2,3,1,0:T(8,128)}, f32[64,1,128,128]{2,3,1,0:T(8,128)}) fusion(s32[128]{0:T(128)S(1)} %iota_multiply_fusion), kind=kLoop, calls=%fused_computation.198 | loop fusion | flops 16777216 | bytes 8389120 | tf_op jit(solution)/shard_map/cos | solution.py:107
  442.0 151.0 %all-to-all-done.2 = f32[2,128,8192]{1,0,2:T(2,128)} async-done(((f32[2,128,8192]{1,0,2:T(2,128)}), f32[2,128,8192]{1,0,2:T(2,128)}, u32[]{:S(2)}, u32[]{:S(2)}) %all-to-all-start.2) | async-done | bytes 8388640 | tf_op jit(solution)/shard_map/all_to_all | solution.py:130
  603.4 14.3 %fusion.42 = f32[64,2,128,256]{3,0,2,1:T(8,128)} fusion(f32[2,128,32,256]{3,2,0,1:T(8,128)} %copy.176, f32[1,32,2,64]{3,1,0,2:T(8,128)S(1)} %get-tuple-element.46, f32[1,32,2,64]{3,1,0,2:T(8,128)S(1)} %get-tuple-element.45), kind=kOutput, calls=%fused_computation.59 | convolution fusion | flops 1610620928 | bytes 25198592 | tf_op jit(solution)/shard_map/paby,pasc->csby/dot_general | solution.py:76
  627.6 27.8 %fusion.8 = f32[64,128,256,1]{2,1,3,0:T(8,128)} fusion(f32[64,2,128,256]{3,0,2,1:T(8,128)} %fusion.42, f32[64,1,128,128]{2,3,1,0:T(8,128)} %get-tuple-element.48, f32[64,1,128,128]{2,3,1,0:T(8,128)} %get-tuple-element.47), kind=kOutput, calls=%fused_computation.8 | convolution fusion | flops 3223322624 | bytes 33554432 | tf_op jit(solution)/shard_map/csby,csbd->cdy/dot_general | solution.py:76
  655.4 27.7 %fusion.6 = f32[64,128,256,1]{2,1,3,0:T(8,128)} fusion(f32[64,2,128,256]{3,0,2,1:T(8,128)} %fusion.45, f32[64,1,128,128]{2,3,1,0:T(8,128)} %get-tuple-element.48, f32[64,1,128,128]{2,3,1,0:T(8,128)} %get-tuple-element.47), kind=kOutput, calls=%fused_computation.6 | convolution fusion | flops 3223322624 | bytes 33554432 | tf_op jit(solution)/shard_map/csby,csbd->cdy/dot_general | solution.py:76
  683.1 15.4 %fusion.16 = f32[64,2,128,256]{3,2,1,0:T(8,128)} fusion(f32[64,128,256,1]{2,1,3,0:T(8,128)} %fusion.6, f32[64,128,256,1]{2,1,3,0:T(8,128)} %fusion.8, f32[64,1,128,128]{2,3,1,0:T(8,128)} %get-tuple-element.48, f32[64,1,128,128]{2,3,1,0:T(8,128)} %get-tuple-element.47), kind=kOutput, calls=%fused_computation.23 | convolution fusion | flops 3229614080 | bytes 41943040 | tf_op jit(solution)/shard_map/cdy,cpfd->cpfy/dot_general | solution.py:76
  698.5 20.8 %fusion.168 = f32[2,32,128,256]{3,1,2,0:T(8,128)S(1)} fusion(f32[64,2,128,256]{3,2,1,0:T(8,128)} %fusion.16, f32[1,64,2,32]{1,3,0,2:T(8,128)S(1)} %get-tuple-element.44, f32[1,64,2,32]{1,3,0,2:T(8,128)S(1)} %get-tuple-element.43), kind=kOutput, calls=%fused_computation.197 | convolution fusion | flops 1610620928 | bytes 25198592 | tf_op jit(solution)/shard_map/cpfy,pcse->sefy/dot_general | solution.py:76
  724.2 23.5 %copy.135 = f32[2,4096,256]{2,0,1:T(2,128)} copy(f32[2,4096,256]{2,1,0:T(8,128)S(1)} %bitcast.252) | data formatting | bytes 16777216 | tf_op jit(solution)/shard_map/reshape | solution.py:126
  759.7 15.1 %fusion.18 = f32[64,2,128,256]{3,2,1,0:T(8,128)} fusion(f32[64,128,256,1]{2,1,3,0:T(8,128)} %fusion.6, f32[64,128,256,1]{2,1,3,0:T(8,128)} %fusion.8, f32[64,1,128,128]{2,3,1,0:T(8,128)} %get-tuple-element.48, f32[64,1,128,128]{2,3,1,0:T(8,128)} %get-tuple-element.47), kind=kOutput, calls=%fused_computation.25 | convolution fusion | flops 3225419776 | bytes 41943040 | tf_op jit(solution)/shard_map/cdy,cpfd->cpfy/dot_general | solution.py:76
  774.8 21.2 %fusion.165 = f32[2,32,128,256]{3,1,2,0:T(8,128)S(1)} fusion(f32[64,2,128,256]{3,2,1,0:T(8,128)} %fusion.18, f32[1,64,2,32]{1,3,0,2:T(8,128)S(1)} %get-tuple-element.44, f32[1,64,2,32]{1,3,0,2:T(8,128)S(1)} %get-tuple-element.43), kind=kOutput, calls=%fused_computation.196 | convolution fusion | flops 1610620928 | bytes 25198592 | tf_op jit(solution)/shard_map/cpfy,pcse->sefy/dot_general | solution.py:76
  800.9 23.4 %copy.125 = f32[2,4096,256]{2,0,1:T(2,128)} copy(f32[2,4096,256]{2,1,0:T(8,128)S(1)} %bitcast.253) | data formatting | bytes 16777216 | tf_op jit(solution)/shard_map/reshape | solution.py:126
  824.3 116.3 %all-to-all-done.4 = f32[2,4096,256]{2,0,1:T(2,128)} async-done(((f32[2,4096,256]{2,0,1:T(2,128)}), f32[2,4096,256]{2,0,1:T(2,128)}, u32[]{:S(2)}, u32[]{:S(2)}) %all-to-all-start.4) | async-done | bytes 8388640 | tf_op jit(solution)/shard_map/all_to_all | solution.py:134
  974.9 158.7 %all-to-all-done.3 = f32[2,4096,256]{2,0,1:T(2,128)} async-done(((f32[2,4096,256]{2,0,1:T(2,128)}), f32[2,4096,256]{2,0,1:T(2,128)}, u32[]{:S(2)}, u32[]{:S(2)}) %all-to-all-start.3) | async-done | bytes 8388640 | tf_op jit(solution)/shard_map/all_to_all | solution.py:134
  1249.7 13.1 copy.142
  1269.2 23.9 %multiply_subtract_fusion.4 = (f32[512,2048]{1,0:T(8,128)}, f32[512,2048]{1,0:T(8,128)}, f32[512,2048]{1,0:T(8,128)}, f32[512,2048]{1,0:T(8,128)}) fusion(f32[512]{0:T(512)S(1)} %multiply_multiply_fusion.3, s32[2048]{0:T(1024)S(1)} %get-tuple-element.50, s32[2048]{0:T(1024)S(1)} %get-tuple-element.49, pred[2048]{0:T(1024)(128)(4,1)S(1)} %fusion.214, ...), kind=kLoop, calls=%fused_computation.188 | loop fusion | flops 102760448 | bytes 16799744 | tf_op jit(solution)/shard_map/sub | solution.py:43
  1293.2 21.0 %multiply_add_fusion.2 = f32[1,2,512,2048]{3,2,1,0:T(8,128)} fusion(f32[1,2,512,2048]{3,2,1,0:T(8,128)} %param.8, f32[1,2,512,2048]{3,2,1,0:T(8,128)} %param.9, f32[1,2,512,2048]{3,2,1,0:T(8,128)} %param.7, f32[1,2,512,2048]{3,2,1,0:T(8,128)} %param.5, f32[512,2048]{1,0:T(8,128)} %get-tuple-element.40, f32[512,2048]{1,0:T(8,128)} %get-tuple-element.41, ...), kind=kLoop, calls=%fused_computation.55 | loop fusion | flops 12582912 | bytes 54525952 | tf_op jit(solution)/shard_map/add | solution.py:190
  1314.1 48.1 %all-to-all-done.5 = f32[2,128,8192]{1,0,2:T(2,128)} async-done(((f32[2,128,8192]{1,0,2:T(2,128)}), f32[2,128,8192]{1,0,2:T(2,128)}, u32[]{:S(2)}, u32[]{:S(2)}) %all-to-all-start.5) | async-done | bytes 8388640 | tf_op jit(solution)/shard_map/all_to_all | solution.py:174
  1362.2 13.2 copy.143
  1375.4 13.7 multiply_add_fusion
  (85 shorter events, 316.7 us)
Async XLA Ops:
  15.4 98.5 %all-to-all-start = ((f32[2,512,2048]{2,0,1:T(2,128)}), f32[2,512,2048]{2,0,1:T(2,128)}, u32[]{:S(2)}, u32[]{:S(2)}) async-start(f32[2,512,2048]{2,0,1:T(2,128)} %bitcast.250), calls=%async_computation | async-start | bytes 16777216 | tf_op jit(solution)/shard_map/all_to_all | solution.py:146
  21.7 126.4 %copy-start.2 = (pred[128]{0:T(512)(128)(4,1)}, pred[128]{0:T(512)(128)(4,1)S(1)}, u32[]{:S(2)}) copy-start(pred[128]{0:T(512)(128)(4,1)S(1)} %multiply_compare_fusion.1) | copy-start | bytes 388
  213.3 186.8 %all-to-all-start.1 = ((f32[2,128,8192]{1,0,2:T(2,128)}), f32[2,128,8192]{1,0,2:T(2,128)}, u32[]{:S(2)}, u32[]{:S(2)}) async-start(f32[2,128,8192]{1,0,2:T(2,128)} %copy.115), calls=%async_computation.1 | async-start | bytes 16777216 | tf_op jit(solution)/shard_map/all_to_all | solution.py:130
  400.1 192.9 %all-to-all-start.2 = ((f32[2,128,8192]{1,0,2:T(2,128)}), f32[2,128,8192]{1,0,2:T(2,128)}, u32[]{:S(2)}, u32[]{:S(2)}) async-start(f32[2,128,8192]{1,0,2:T(2,128)} %copy.119), calls=%async_computation.2 | async-start | bytes 16777216 | tf_op jit(solution)/shard_map/all_to_all | solution.py:130
  603.4 14.3 %copy-start.1 = (f32[2,128,32,256]{3,2,0,1:T(8,128)S(1)}, f32[2,128,32,256]{3,2,0,1:T(8,128)}, u32[]{:S(2)}) copy-start(f32[2,128,32,256]{3,2,0,1:T(8,128)} %copy.177) | copy-start | bytes 25165828
  747.7 192.9 %all-to-all-start.4 = ((f32[2,4096,256]{2,0,1:T(2,128)}), f32[2,4096,256]{2,0,1:T(2,128)}, u32[]{:S(2)}, u32[]{:S(2)}) async-start(f32[2,4096,256]{2,0,1:T(2,128)} %copy.135), calls=%async_computation.4 | async-start | bytes 16777216 | tf_op jit(solution)/shard_map/all_to_all | solution.py:134
  824.3 129.7 %copy-start.3 = (pred[128]{0:T(512)(128)(4,1)S(1)}, pred[128]{0:T(512)(128)(4,1)}, u32[]{:S(2)}) copy-start(pred[128]{0:T(512)(128)(4,1)} %copy-done.2) | copy-start | bytes 388
  824.3 129.7 %copy-start.4 = (f32[128]{0:T(128)S(1)}, f32[128]{0:T(128)}, u32[]{:S(2)}) copy-start(f32[128]{0:T(128)} %get-tuple-element.52) | copy-start | bytes 1540
  824.3 129.7 %copy-start.5 = (f32[128]{0:T(128)S(1)}, f32[128]{0:T(128)}, u32[]{:S(2)}) copy-start(f32[128]{0:T(128)} %get-tuple-element.54) | copy-start | bytes 1540
  940.6 193.0 %all-to-all-start.3 = ((f32[2,4096,256]{2,0,1:T(2,128)}), f32[2,4096,256]{2,0,1:T(2,128)}, u32[]{:S(2)}, u32[]{:S(2)}) async-start(f32[2,4096,256]{2,0,1:T(2,128)} %copy.125), calls=%async_computation.3 | async-start | bytes 16777216 | tf_op jit(solution)/shard_map/all_to_all | solution.py:134
  1150.1 6.8 copy-start
  1262.8 99.4 %all-to-all-start.5 = ((f32[2,128,8192]{1,0,2:T(2,128)}), f32[2,128,8192]{1,0,2:T(2,128)}, u32[]{:S(2)}, u32[]{:S(2)}) async-start(f32[2,128,8192]{1,0,2:T(2,128)} %copy.142), calls=%async_computation.5 | async-start | bytes 16777216 | tf_op jit(solution)/shard_map/all_to_all | solution.py:174
where the time goes:
time: 1410 us; the launch traced here: 1390 us
  waiting for transfers between devices  701 us (50%)
  local copies, waits for them, and re-layouts  285 us (20%)
  matrix products  211 us (15%)
  other arithmetic  137 us (10%)
  starting transfers between devices  55.1 us (4%)
    all_to_all x2, waiting for transfers between devices, to_columns(): lax.all_to_all(lines, ('col', 'row'), split_axis=2, concat_axis=1, tiled=...  287 us
    all_to_all x2, waiting for transfers between devices, to_lines(): lax.all_to_all(columns, ('col', 'row'), split_axis=1, concat_axis=2, tile...  275 us
    dot_general x16, matrix products, product(): return jnp.einsum(equation, left, right, precision=lax.Precision.HIGH)  211 us
    all_to_all x1, waiting for transfers between devices, nonlinear(): lax.all_to_all(section_field, 'row', split_axis=1, concat_axis=2, tiled=T...  90.1 us
    reshape x2, local copies, waits for them, and re-layouts, lines_inverse(): return second.reshape((parts, count_k, length))  63 us
    all_to_all x1, waiting for transfers between devices, nonlinear(): return lax.all_to_all(term, 'row', split_axis=2, concat_axis=1, tiled=True)  48.1 us
    reshape x2, local copies, waits for them, and re-layouts, columns_forward(): return second.reshape((2, half_count * count_d, count_y))  46.9 us
    all_to_all x4, local copies, waits for them, and re-layouts, to_lines(): lax.all_to_all(columns, ('col', 'row'), split_axis=1, concat_axis=2, tile...  32.6 us
  transfers between devices with their start and end apart: 6, of which 6 were waited for; matrix products, arithmetic and copies ran while one was open for 15% of the time, Pallas kernels for 0%

commit v1 on v0

--- a/solution.py
+++ b/solution.py
@@ -1,8 +1,11 @@
+import functools
 import math
 
 import jax
 import jax.numpy as jnp
 from jax import lax
+from jax.experimental import pallas as pl
+from jax.experimental.pallas import tpu as pltpu
 from jax.sharding import PartitionSpec as P
 
 RADIX = 128
@@ -196,17 +199,683 @@
     return linear + weight_c * section_term
 
 
+LANES = 128
+SUBL = 8
+HALF = 64
+
+
+def plan_of(length, rows, cols, block_x, block_y):
+    if length != LANES * HALF or rows != 4 or block_x % (rows * SUBL) or block_y * rows != length:
+        return None
+    kept = (length - 1) // 3 + 1
+    stride = rows * SUBL
+    groups = block_x // stride
+    own = [min(groups, max(0, -(-(kept - c * block_x) // stride))) for c in range(cols)]
+    slots = -(-sum(own) // cols)
+    extra = groups - slots
+    donors = [c for c in range(cols) if own[c] == groups]
+    if extra <= 0 or 2 * extra > slots or any(slots < own[c] < groups for c in range(cols)):
+        return None
+    takers = [c for c in range(cols) if own[c] + extra <= slots]
+    first = [(c, 0) for c in takers]
+    second = [(c, 1) for c in takers if own[c] == 0]
+    places = first + second
+    if len(donors) > len(places):
+        return None
+    order = donors[-1:] + donors[:-1]
+    moves = [(donor, taker, turn) for donor, (taker, turn) in zip(order, places)]
+    low = (kept + LANES - 1) // LANES
+    high = HALF - (length - kept + 1) // LANES
+    if low != high or low % 2 or low > HALF // 2:
+        return None
+    per = low // 2
+    home_tiles = block_y // LANES
+    if not per < home_tiles < low:
+        return None
+    return dict(
+        kept=kept, stride=stride, groups=groups, own=own, slots=slots, extra=extra,
+        moves=moves, low=low, per=per, home=home_tiles, rows=rows, cols=cols,
+        block_x=block_x, block_y=block_y, length=length,
+    )
+
+
+def home_of(plan, group):
+    per_block = plan["block_x"] // SUBL
+    if group * SUBL >= plan["kept"]:
+        return None
+    col, inside = divmod(group, per_block)
+    slot = inside // plan["rows"]
+    if slot < plan["slots"]:
+        return col, slot
+    for donor, taker, turn in plan["moves"]:
+        if donor == col:
+            start = plan["slots"] - plan["extra"] if turn == 0 else 0
+            return taker, start + slot - plan["slots"]
+    raise ValueError("no place")
+
+
+def line_info(plan):
+    rows = []
+    slots, extra = plan["slots"], plan["extra"]
+    for col in range(plan["cols"]):
+        base = [col * plan["block_x"] + slot * plan["stride"] for slot in range(slots)]
+        flags = [0, 0]
+        for donor, taker, turn in plan["moves"]:
+            if taker == col:
+                flags[turn] = 1
+                start = slots - extra if turn == 0 else 0
+                for step in range(extra):
+                    base[start + step] = donor * plan["block_x"] + (slots + step) * plan["stride"]
+        rows.append(base + flags)
+    return rows
+
+
+def cadd(a, b):
+    if a is None:
+        return b
+    if b is None:
+        return a
+    return (a[0] + b[0], a[1] + b[1])
+
+
+def csub(a, b):
+    if b is None:
+        return a
+    if a is None:
+        return (-b[0], -b[1])
+    return (a[0] - b[0], a[1] - b[1])
+
+
+def cturn(a, step, period, sign):
+    if a is None:
+        return None
+    step = step * sign % period
+    if step == 0:
+        return a
+    if 4 * step == period:
+        return (-a[1], a[0])
+    if 2 * step == period:
+        return (-a[0], -a[1])
+    if 4 * step == 3 * period:
+        return (a[1], -a[0])
+    angle = 2.0 * math.pi * step / period
+    cosine, sine_part = math.cos(angle), math.sin(angle)
+    if 8 * step % period == 0:
+        size = math.sqrt(0.5)
+        sign_c, sign_s = (1 if cosine > 0 else -1), (1 if sine_part > 0 else -1)
+        real = a[0] - a[1] if sign_c == sign_s else a[0] + a[1]
+        imag = a[0] + a[1] if sign_c == sign_s else a[1] - a[0]
+        return (real * (sign_c * size), imag * (sign_c * size))
+    return (a[0] * cosine - a[1] * sine_part, a[0] * sine_part + a[1] * cosine)
+
+
+def butterflies(values, sign, need):
+    count = len(values)
+    if all(v is None for v in values):
+        return {k: None for k in need}
+    if count == 1:
+        return {k: values[0] for k in need}
+    half = count // 2
+    sub = sorted({k % half for k in need})
+    even = butterflies(values[0::2], sign, sub)
+    odd = butterflies(values[1::2], sign, sub)
+    wanted = set(need)
+    out = {}
+    for k in sub:
+        turned = cturn(odd[k], k, count, sign)
+        if k in wanted:
+            out[k] = cadd(even[k], turned)
+        if k + half in wanted:
+            out[k + half] = csub(even[k], turned)
+    return out
+
+
+def halves(values):
+    high = values.astype(jnp.bfloat16)
+    return high, (values - high.astype(jnp.float32)).astype(jnp.bfloat16)
+
+
+def dot3(left, right):
+    lh, ll = left
+    rh, rl = right
+    def mm(a, b):
+        return jnp.dot(a, b, preferred_element_type=jnp.float32)
+    return mm(lh, rh) + (mm(ll, rh) + mm(lh, rl))
+
+
+def tile_of(plan, a):
+    low = plan["low"]
+    t = a if a < low else a - (HALF - 2 * low)
+    return t // plan["per"], (t % plan["per"]) * LANES
+
+
+def kept_tiles(plan):
+    low = plan["low"]
+    return list(range(low)) + list(range(HALF - low, HALF))
+
+
+def sublane_iota():
+    return lax.broadcasted_iota(jnp.int32, (SUBL, LANES), 0)
+
+
+def lane_iota():
+    return lax.broadcasted_iota(jnp.int32, (SUBL, LANES), 1)
+
+
+def keep_of(plan, wave_x, wave_y):
+    return (3 * wave_x < plan["length"]) & (3 * jnp.abs(wave_y) < plan["length"])
+
+
+def lines_in_kernel(plan, parity, info, own, mv1, mv2, turn, wh, wl, out, scr):
+    slots, extra, length = plan["slots"], plan["extra"], plan["length"]
+    j = pl.program_id(0)
+    use1 = (info[slots] == 1) & (j >= slots - extra)
+    use2 = (info[slots + 1] == 1) & (j < extra)
+    wave_x = info[j] + sublane_iota()
+    kx = wave_x.astype(jnp.float32)
+    doubled = jnp.where(wave_x == 0, 1.0, 2.0) * (length / 9.0)
+    step = wave_scale / length
+    lane = lane_iota()
+    for field in range(2):
+        tiles = {}
+        for a in kept_tiles(plan):
+            r, off = tile_of(plan, a)
+            wave_y = lane + (LANES * a - (length if a >= HALF // 2 else 0))
+            square = (wave_x * wave_x + wave_y * wave_y)
+            value = doubled / jnp.maximum(square, 1).astype(jnp.float32)
+            factor = jnp.where(keep_of(plan, wave_x, wave_y), value, 0.0)
+            if field == 0:
+                factor = factor * (step * wave_y.astype(jnp.float32))
+            else:
+                factor = factor * (-step * kx)
+            parts = []
+            for p in range(2):
+                at = (r, p, slice(None), slice(off, off + LANES))
+                parts.append(jnp.where(use1, mv1[at], jnp.where(use2, mv2[at], own[at])))
+            tiles[a] = (-factor * parts[1], factor * parts[0])
+        mixed = []
+        for a in range(HALF // 2):
+            x0, x1 = tiles.get(a), tiles.get(a + HALF // 2)
+            if parity == 0:
+                mixed.append(cadd(x0, x1))
+            else:
+                mixed.append(cturn(csub(x0, x1), a, HALF, 1))
+        result = butterflies(mixed, 1, range(HALF // 2))
+        for e in range(HALF // 2):
+            re, im = result[e]
+            cosine, sine_part = turn[e, 0:1, :], turn[e, 1:2, :]
+            at = slice(SUBL * e, SUBL * (e + 1))
+            scr[at, 0:LANES] = re * cosine - im * sine_part
+            scr[at, LANES:] = re * sine_part + im * cosine
+        spread = dot3(halves(scr[...]), (wh[...], wl[...]))
+        for s in range(2):
+            out[:, field, s] = spread[:, s * LANES:(s + 1) * LANES].reshape(
+                HALF // 2, SUBL, LANES
+            )
+
+
+def lines_in(plan, parity, info, own, mv1, mv2, turn, table):
+    slots, extra, rows = plan["slots"], plan["extra"], plan["rows"]
+    width = plan["per"] * LANES
+    block = (rows, 2, SUBL, width)
+    devices = rows * plan["cols"]
+    whole = lambda shape: pl.BlockSpec(shape, lambda j: (0,) * len(shape))
+    return pl.pallas_call(
+        functools.partial(lines_in_kernel, plan, parity),
+        grid=(slots,),
+        in_specs=[
+            pl.BlockSpec(memory_space=pltpu.SMEM),
+            pl.BlockSpec(block, lambda j: (0, 0, j, 0)),
+            pl.BlockSpec(block, lambda j: (0, 0, jnp.maximum(j - (slots - extra), 0), 0)),
+            pl.BlockSpec(block, lambda j: (0, 0, jnp.minimum(j, extra - 1), 0)),
+            whole((HALF // 2, 2, LANES)),
+            whole((2 * LANES, 2 * LANES)),
+            whole((2 * LANES, 2 * LANES)),
+        ],
+        out_specs=pl.BlockSpec((devices, 2, 2, SUBL, LANES), lambda j: (0, 0, 0, j, 0)),
+        out_shape=jax.ShapeDtypeStruct((devices, 2, 2, slots * SUBL, LANES), jnp.float32),
+        scratch_shapes=[pltpu.VMEM((HALF // 2 * SUBL, 2 * LANES), jnp.float32)],
+        compiler_params=pltpu.CompilerParams(vmem_limit_bytes=50 << 20),
+        cost_estimate=pl.CostEstimate(flops=4 << 30, bytes_accessed=16 << 20, transcendentals=0),
+        name="lines_in",
+    )(info, own, mv1, mv2, turn, *table)
+
+
+def columns_kernel(plan, src, th, tl, fh, fl, out, mid):
+    rows = plan["rows"]
+    low = plan["low"]
+    per_tile = LANES // SUBL
+    quarter = per_tile // rows
+    inside = [[home_of(plan, a * per_tile + q * rows) for a in range(low)] for q in range(quarter)]
+    used = {place for line in inside for place in line if place}
+
+    @pl.loop(0, 2 * rows)
+    def _(i):
+        r = i % rows
+        field = i // rows
+        lanes = pl.ds(pl.multiple_of(field * LANES, LANES), LANES)
+        for q in range(quarter):
+            values = []
+            for a in range(HALF):
+                place = inside[q][a] if a < low else None
+                if place is None:
+                    values.append(None)
+                    continue
+                at = pl.ds(place[1] * SUBL, SUBL)
+                dev = place[0] * rows + r
+                values.append((src[dev, field, 0, at, :], src[dev, field, 1, at, :]))
+            result = butterflies(values, 1, range(HALF))
+            base = pl.multiple_of((q * rows + r) * SUBL, SUBL)
+            for c in range(HALF):
+                mid[c, pl.ds(base, SUBL), lanes] = result[c][0]
+                mid[c, pl.ds(LANES + base, SUBL), lanes] = result[c][1]
+
+    @pl.loop(0, HALF)
+    def _(c):
+        grid = dot3((th[c], tl[c]), halves(mid[c]))
+        u, v = grid[:, :LANES], grid[:, LANES:]
+        pair = jnp.concatenate([u * v, (v - u) * (v + u)], axis=1)
+        mid[c] = dot3((fh[c], fl[c]), halves(pair))
+
+    @pl.loop(0, 2 * rows)
+    def _(i):
+        r = i % rows
+        field = i // rows
+        lanes = pl.ds(pl.multiple_of(field * LANES, LANES), LANES)
+        for q in range(quarter):
+            base = pl.multiple_of((q * rows + r) * SUBL, SUBL)
+            values = [
+                (mid[c, pl.ds(base, SUBL), lanes], mid[c, pl.ds(LANES + base, SUBL), lanes])
+                for c in range(HALF)
+            ]
+            need = [a for a in range(low) if inside[q][a]]
+            result = butterflies(values, -1, need)
+            for a in need:
+                place = inside[q][a]
+                at = pl.ds(place[1] * SUBL, SUBL)
+                dev = place[0] * rows + r
+                out[dev, field, 0, at, :] = result[a][0]
+                out[dev, field, 1, at, :] = result[a][1]
+        for col in range(plan["cols"]):
+            for slot in range(plan["slots"]):
+                if (col, slot) not in used:
+                    for p in range(2):
+                        out[col * rows + r, field, p, pl.ds(slot * SUBL, SUBL), :] = jnp.zeros(
+                            (SUBL, LANES), jnp.float32
+                        )
+
+
+def columns(plan, spread, tables):
+    return pl.pallas_call(
+        functools.partial(columns_kernel, plan),
+        in_specs=[pl.BlockSpec(memory_space=pltpu.VMEM)] * 5,
+        out_specs=pl.BlockSpec(memory_space=pltpu.VMEM),
+        out_shape=jax.ShapeDtypeStruct(spread.shape, jnp.float32),
+        scratch_shapes=[pltpu.VMEM((HALF, 2 * LANES, 2 * LANES), jnp.float32)],
+        compiler_params=pltpu.CompilerParams(vmem_limit_bytes=60 << 20),
+        cost_estimate=pl.CostEstimate(flops=16 << 30, bytes_accessed=30 << 20, transcendentals=0),
+        name="columns",
+    )(spread, *tables)
+
+
+def lines_out_kernel(plan, info, got0, got1, turn, wh, wl, own, mv1, mv2, scr, acc):
+    slots, extra, length = plan["slots"], plan["extra"], plan["length"]
+    j = pl.program_id(0)
+    wave_x = info[j] + sublane_iota()
+    step = wave_scale / length
+    kappa_x = step * wave_x.astype(jnp.float32)
+    lane = lane_iota()
+    tiles = kept_tiles(plan)
+    rows = HALF // 2 * SUBL
+    for field in range(2):
+        for parity, got in enumerate((got0, got1)):
+            both = jnp.concatenate(
+                [got[:, field, s].reshape(rows, LANES) for s in range(2)], axis=1
+            )
+            scr[parity] = dot3(halves(both), (wh[...], wl[...]))
+        values = []
+        for c in range(HALF):
+            e, parity = c // 2, c % 2
+            at = slice(SUBL * e, SUBL * (e + 1))
+            re, im = scr[parity, at, 0:LANES], scr[parity, at, LANES:]
+            cosine, sine_part = turn[parity, e, 0:1, :], turn[parity, e, 1:2, :]
+            values.append((re * cosine + im * sine_part, im * cosine - re * sine_part))
+        result = butterflies(values, -1, tiles)
+        for t, a in enumerate(tiles):
+            wave_y = lane + (LANES * a - (length if a >= HALF // 2 else 0))
+            kappa_y = step * wave_y.astype(jnp.float32)
+            keep = keep_of(plan, wave_x, wave_y)
+            if field == 0:
+                weight = (kappa_x * kappa_x - kappa_y * kappa_y) * (1.0 / length)
+            else:
+                weight = kappa_x * kappa_y * (1.0 / length)
+            r, off = tile_of(plan, a)
+            for p in range(2):
+                value = jnp.where(keep, weight * result[a][p], 0.0)
+                if field == 0:
+                    acc[t, p] = value
+                else:
+                    own[r, p, :, off:off + LANES] = acc[t, p] + value
+
+    @pl.when(j < extra)
+    def _():
+        mv2[...] = own[...]
+
+    @pl.when(j >= slots - extra)
+    def _():
+        mv1[...] = own[...]
+
+
+def lines_out(plan, info, got0, got1, turn, table):
+    slots, extra, rows = plan["slots"], plan["extra"], plan["rows"]
+    width = plan["per"] * LANES
+    block = (rows, 2, SUBL, width)
+    devices = rows * plan["cols"]
+    whole = lambda shape: pl.BlockSpec(shape, lambda j: (0,) * len(shape))
+    got_spec = pl.BlockSpec((devices, 2, 2, SUBL, LANES), lambda j: (0, 0, 0, j, 0))
+    lines = lambda n: jax.ShapeDtypeStruct((rows, 2, n * SUBL, width), jnp.float32)
+    return pl.pallas_call(
+        functools.partial(lines_out_kernel, plan),
+        grid=(slots,),
+        in_specs=[
+            pl.BlockSpec(memory_space=pltpu.SMEM),
+            got_spec,
+            got_spec,
+            whole((2, HALF // 2, 2, LANES)),
+            whole((2 * LANES, 2 * LANES)),
+            whole((2 * LANES, 2 * LANES)),
+        ],
+        out_specs=[
+            pl.BlockSpec(block, lambda j: (0, 0, j, 0)),
+            pl.BlockSpec(block, lambda j: (0, 0, jnp.maximum(j - (slots - extra), 0), 0)),
+            pl.BlockSpec(block, lambda j: (0, 0, jnp.minimum(j, extra - 1), 0)),
+        ],
+        out_shape=[lines(slots), lines(extra), lines(extra)],
+        scratch_shapes=[
+            pltpu.VMEM((2, HALF // 2 * SUBL, 2 * LANES), jnp.float32),
+            pltpu.VMEM((4 * plan["per"], 2, SUBL, LANES), jnp.float32),
+        ],
+        compiler_params=pltpu.CompilerParams(vmem_limit_bytes=50 << 20),
+        cost_estimate=pl.CostEstimate(flops=8 << 30, bytes_accessed=22 << 20, transcendentals=0),
+        name="lines_out",
+    )(info, got0, got1, turn, *table)
+
+
+def pack_kernel(plan, info, field, got, own, mv):
+    per, home, slots, rows = plan["per"], plan["home"], plan["slots"], plan["rows"]
+    j = pl.program_id(0)
+    more = home - per
+    width, full = per * LANES, home * LANES
+    less = width - more * LANES
+
+    def put(dest):
+        for p in range(2):
+            for r in range(rows):
+                at = slice(r * SUBL, (r + 1) * SUBL)
+
+                @pl.when(info[0] == 0)
+                def _():
+                    dest[r, p] = field[0, p, at, :width]
+
+                @pl.when(info[0] == 1)
+                def _():
+                    dest[r, p, :, :more * LANES] = got[p, at, :]
+                    dest[r, p, :, more * LANES:] = field[0, p, at, :less]
+
+                @pl.when(info[0] == 2)
+                def _():
+                    dest[r, p, :, :less] = field[0, p, at, full - less:]
+                    dest[r, p, :, less:] = got[p, at, :]
+
+                @pl.when(info[0] == 3)
+                def _():
+                    dest[r, p] = field[0, p, at, full - width:]
+
+    @pl.when(j < slots)
+    def _():
+        put(own)
+
+    @pl.when(j >= slots)
+    def _():
+        put(mv)
+
+
+def pack(plan, where, field, member, got):
+    slots, extra, rows, groups = plan["slots"], plan["extra"], plan["rows"], plan["groups"]
+    width = plan["per"] * LANES
+    more = (plan["home"] - plan["per"]) * LANES
+    block = (rows, 2, SUBL, width)
+    lines = lambda n: jax.ShapeDtypeStruct((rows, 2, n * SUBL, width), jnp.float32)
+    return pl.pallas_call(
+        functools.partial(pack_kernel, plan),
+        grid=(groups,),
+        in_specs=[
+            pl.BlockSpec(memory_space=pltpu.SMEM),
+            pl.BlockSpec((1, 2, plan["stride"], plan["block_y"]), lambda j: (member, 0, j, 0)),
+            pl.BlockSpec((2, plan["stride"], more), lambda j: (0, j, 0)),
+        ],
+        out_specs=[
+            pl.BlockSpec(block, lambda j: (0, 0, jnp.minimum(j, slots - 1), 0)),
+            pl.BlockSpec(block, lambda j: (0, 0, jnp.maximum(j - slots, 0), 0)),
+        ],
+        out_shape=[lines(slots), lines(extra)],
+        compiler_params=pltpu.CompilerParams(vmem_limit_bytes=32 << 20),
+        cost_estimate=pl.CostEstimate(flops=1 << 24, bytes_accessed=14 << 20, transcendentals=0),
+        name="pack",
+    )(where, field, got)
+
+
+def unpack_kernel(plan, info, own, mv, got_own, got_mv, linear, weight, out, term):
+    per, home, slots, rows = plan["per"], plan["home"], plan["slots"], plan["rows"]
+    j = pl.program_id(0)
+    more = (home - per) * LANES
+    width, full = per * LANES, home * LANES
+    less = width - more
+    keep_x = info[1] + j * plan["stride"]
+
+    def put(lines, got):
+        for p in range(2):
+            for r in range(rows):
+                at = slice(r * SUBL, (r + 1) * SUBL)
+
+                @pl.when(info[0] == 0)
+                def _():
+                    term[p, at, :width] = lines[r, p]
+                    term[p, at, width:] = got[r, p]
+
+                @pl.when(info[0] == 1)
+                def _():
+                    term[p, at, :less] = lines[r, p, :, more:]
+                    term[p, at, less:] = jnp.zeros((SUBL, full - less), jnp.float32)
+
+                @pl.when(info[0] == 2)
+                def _():
+                    term[p, at, full - less:] = lines[r, p, :, :less]
+                    term[p, at, :full - less] = jnp.zeros((SUBL, full - less), jnp.float32)
+
+                @pl.when(info[0] == 3)
+                def _():
+                    term[p, at, full - width:] = lines[r, p]
+                    term[p, at, :full - width] = got[r, p]
+
+    @pl.when(j < slots)
+    def _():
+        put(own, got_own)
+
+    @pl.when(j >= slots)
+    def _():
+        put(mv, got_mv)
+
+    wave_x = keep_x + lax.broadcasted_iota(jnp.int32, (plan["stride"], full), 0)
+    keep = 3 * wave_x < plan["length"]
+    for p in range(2):
+        out[p] = linear[p] + jnp.where(keep, weight[...] * term[p], 0.0)
+
+
+def unpack(plan, where, own, mv, got_own, got_mv, linear, weight):
+    slots, rows, groups = plan["slots"], plan["rows"], plan["groups"]
+    width = plan["per"] * LANES
+    more = (plan["home"] - plan["per"]) * LANES
+    own_at = lambda j: (0, 0, jnp.minimum(j, slots - 1), 0)
+    mv_at = lambda j: (0, 0, jnp.maximum(j - slots, 0), 0)
+    rowed = pl.BlockSpec((2, plan["stride"], plan["block_y"]), lambda j: (0, j, 0))
+    return pl.pallas_call(
+        functools.partial(unpack_kernel, plan),
+        grid=(groups,),
+        in_specs=[
+            pl.BlockSpec(memory_space=pltpu.SMEM),
+            pl.BlockSpec((rows, 2, SUBL, width), own_at),
+            pl.BlockSpec((rows, 2, SUBL, width), mv_at),
+            pl.BlockSpec((rows, 2, SUBL, more), own_at),
+            pl.BlockSpec((rows, 2, SUBL, more), mv_at),
+            rowed,
+            pl.BlockSpec((plan["stride"], plan["block_y"]), lambda j: (j, 0)),
+        ],
+        out_specs=rowed,
+        out_shape=jax.ShapeDtypeStruct(linear.shape, jnp.float32),
+        scratch_shapes=[pltpu.VMEM((2, plan["stride"], plan["block_y"]), jnp.float32)],
+        compiler_params=pltpu.CompilerParams(vmem_limit_bytes=32 << 20),
+        cost_estimate=pl.CostEstimate(flops=1 << 24, bytes_accessed=34 << 20, transcendentals=0),
+        name="unpack",
+    )(where, own, mv, got_own, got_mv, linear, weight)
+
+
+def split_table(values):
+    high = lax.reduce_precision(values, 8, 7)
+    return high.astype(jnp.bfloat16), (values - high).astype(jnp.bfloat16)
+
+
+def angle_pair(rows, cols, period):
+    row_ids = lax.broadcasted_iota(jnp.int32, (rows, cols), 0)
+    col_ids = lax.broadcasted_iota(jnp.int32, (rows, cols), 1)
+    angles = 2.0 * math.pi / period * (row_ids * col_ids % period).astype(jnp.float32)
+    return jnp.cos(angles), jnp.sin(angles)
+
+
+def lane_table(sign):
+    cosine, sine_part = angle_pair(LANES, LANES, LANES)
+    sine_part = sign * sine_part
+    return split_table(
+        jnp.concatenate(
+            [
+                jnp.concatenate([cosine, sine_part], axis=1),
+                jnp.concatenate([-sine_part, cosine], axis=1),
+            ],
+            axis=0,
+        )
+    )
+
+
+def turns(length):
+    cosine, sine_part = angle_pair(HALF, LANES, length)
+    both = jnp.stack([cosine, sine_part], axis=1).reshape(HALF // 2, 2, 2, LANES)
+    return jnp.swapaxes(both, 0, 1)
+
+
+def column_tables(length):
+    cos_b, sin_b = angle_pair(LANES, LANES, LANES)
+    cos_c, sin_c = angle_pair(HALF, LANES, length)
+
+    def both(turn_shape, axis):
+        ct, st = cos_c.reshape(turn_shape), sin_c.reshape(turn_shape)
+        cosine = ct * cos_b - st * sin_b
+        sine_part = st * cos_b + ct * sin_b
+        return split_table(jnp.concatenate([cosine, -sine_part], axis=axis))
+
+    inverse = both((HALF, 1, LANES), 2)
+    forward = both((HALF, LANES, 1), 1)
+    return inverse + forward
+
+
+def fast_term(plan, member, section_field, finish):
+    rows, cols, length = plan["rows"], plan["cols"], plan["length"]
+    slots, per, home = plan["slots"], plan["per"], plan["home"]
+    row = lax.axis_index("row")
+    col = lax.axis_index("col")
+    where = jnp.stack([row, col * plan["block_x"]]).astype(jnp.int32)
+    info = jnp.asarray(line_info(plan), jnp.int32)[col]
+    info = info + jnp.where(jnp.arange(slots + 2) < slots, row * SUBL, 0).astype(jnp.int32)
+    more = (home - per) * LANES
+    edge = jnp.where(
+        row < rows // 2, section_field[member, :, :, per * LANES:],
+        section_field[member, :, :, :more],
+    )
+    got = lax.ppermute(edge, "row", [(0, 1), (3, 2)])
+    own, moved = pack(plan, where, section_field, member, got)
+
+    def swap(lines):
+        return lax.all_to_all(lines, "row", split_axis=0, concat_axis=0, tiled=True)
+
+    def across(lines):
+        return lax.all_to_all(lines, ("col", "row"), split_axis=0, concat_axis=0, tiled=True)
+
+    pairs = [[(d, t) for d, t, turn in plan["moves"] if turn == k] for k in range(2)]
+    moved1 = lax.ppermute(moved, "col", pairs[0])
+    moved2 = lax.ppermute(moved, "col", pairs[1])
+    own = swap(own)
+    moved1 = swap(moved1)
+    moved2 = swap(moved2)
+    turn = turns(length)
+    table = lane_table(1.0)
+    spread = [
+        across(lines_in(plan, parity, info, own, moved1, moved2, turn[parity], table))
+        for parity in range(2)
+    ]
+    tables = column_tables(length)
+    back = [across(columns(plan, part, tables)) for part in spread]
+    own, moved1, moved2 = lines_out(plan, info, *back, turn, lane_table(-1.0))
+    own = swap(own)
+    moved1 = swap(moved1)
+    moved2 = swap(moved2)
+    flip = [[(t, d) for d, t in group] for group in pairs]
+    moved = lax.ppermute(moved1, "col", flip[0]) + lax.ppermute(moved2, "col", flip[1])
+
+    def edge_of(lines):
+        side = jnp.where(row < rows // 2, lines[..., :more], lines[..., per * LANES - more:])
+        return lax.ppermute(side, "row", [(1, 0), (2, 3)])
+
+    return finish(where, own, moved, edge_of(own), edge_of(moved))
+
+
+def fast_device(plan, start_field, section_field, start_term, first_term, second_term):
+    wave_x, wave_y = positions(
+        (plan["block_x"], plan["block_y"]),
+        lax.axis_index("col") * plan["block_x"],
+        lax.axis_index("row") * plan["block_y"],
+        plan["length"],
+    )
+    damping, weight_a, weight_b, weight_c = section_weights(wave_x, wave_y, plan["length"])[:4]
+    linear = (
+        damping * start_field
+        + weight_a * start_term
+        + 2.0 * weight_b * (first_term + second_term)
+    )
+    linear, weight_c = lax.optimization_barrier((linear, weight_c))
+    out = []
+    for member in range(start_field.shape[0]):
+        out.append(
+            fast_term(
+                plan, member, section_field,
+                lambda where, *parts: unpack(plan, where, *parts, linear[member], weight_c),
+            )
+        )
+    return jnp.stack(out)
+
+
 def solution(mesh):
+    rows, cols = mesh.shape["row"], mesh.shape["col"]
+
+    def body(start_field, *rest):
+        block_x, block_y = start_field.shape[2], start_field.shape[3]
+        plan = plan_of(block_y * rows, rows, cols, block_x, block_y)
+        if plan is None:
+            return per_device(start_field, *rest)
+        return fast_device(plan, start_field, *rest)
+
     return jax.shard_map(
-        per_device,
+        body,
         mesh=mesh,
-        in_specs=(
-            P(None, None, "col", "row"),
-            P(None, None, "col", "row"),
-            P(None, None, "col", "row"),
-            P(None, None, "col", "row"),
-            P(None, None, "col", "row"),
-        ),
+        in_specs=(P(None, None, "col", "row"),) * 5,
         out_specs=P(None, None, "col", "row"),
         check_vma=False,
     )

time: 1410 us -> 891 us (0.63)
  waiting for transfers between devices: 701 us -> 396 us
  local copies, waits for them, and re-layouts: 285 us -> 12.1 us
  matrix products: 211 us -> 0 us
  Pallas kernels: 0 us -> 177 us
  blocking collectives: 0 us -> 162 us
  other arithmetic: 137 us -> 70.1 us
    all_to_all x6 -> x8, waiting for transfers between devices: 701 us -> 315 us  [the longest x3 235 us: across(): lax.all_to_all(lines, ('col', 'row'), split_axis=0, concat_axis=0, tiled=...]
    dot_general x16 -> x0, matrix products: 211 us -> none  [product(): return jnp.einsum(equation, left, right, precision=lax.Precision.HIGH)]
    pallas_call x0 -> x7, Pallas kernels: none -> 177 us  [the longest x2 114 us: columns(): pl.pallas_call(functools.partial(columns_kernel, plan), in_specs=[pl.Bloc...]
    all_to_all x0 -> x2, blocking collectives: none -> 162 us  [the longest x1 136 us: across(): lax.all_to_all(lines, ('col', 'row'), split_axis=0, concat_axis=0, tiled=...]
    reshape x6 -> x0, local copies, waits for them, and re-layouts: 129 us -> none  [the longest x2 63 us: lines_inverse(): return second.reshape((parts, count_k, length))]
    ppermute x0 -> x7, waiting for transfers between devices: none -> 81.2 us  [the longest x1 75.5 us: fast_term(): moved2 = lax.ppermute(moved, 'col', pairs[1])]
    all_to_all x8 -> x0, local copies, waits for them, and re-layouts: 78.8 us -> none  [the longest x4 32.6 us: to_lines(): lax.all_to_all(columns, ('col', 'row'), split_axis=1, concat_axis=2, tile...]
    add x3, other arithmetic: 47.2 us -> 23.9 us  [the longest x1 21 us: fast_device(): damping * start_field + weight_a * start_term]
  transfers between devices with their start and end apart: 6 -> 15, of which waited for: 6 -> 9; matrix products, arithmetic and copies ran while one was open for 15% -> 7% of each run, Pallas kernels for 0% -> 14%
where the time goes in v1:
time: 891 us; the launch traced here: 883 us
  waiting for transfers between devices  396 us (44%)
  Pallas kernels  177 us (20%)
  blocking collectives  162 us (18%)
  other arithmetic  70.1 us (8%)
  starting transfers between devices  66.1 us (7%)
  local copies, waits for them, and re-layouts  12.1 us (1%)
    all_to_all x3, waiting for transfers between devices, across(): lax.all_to_all(lines, ('col', 'row'), split_axis=0, concat_axis=0, tiled=...  235 us
    all_to_all x1, blocking collectives, across(): lax.all_to_all(lines, ('col', 'row'), split_axis=0, concat_axis=0, tiled=...  136 us
    pallas_call x2, Pallas kernels, columns(): pl.pallas_call(functools.partial(columns_kernel, plan), in_specs=[pl.Bloc...  114 us
    all_to_all x5, waiting for transfers between devices, swap(): return lax.all_to_all(lines, 'row', split_axis=0, concat_axis=0, tiled=True)  79.9 us
    ppermute x1, waiting for transfers between devices, fast_term(): moved2 = lax.ppermute(moved, 'col', pairs[1])  75.5 us
    all_to_all x1, blocking collectives, swap(): return lax.all_to_all(lines, 'row', split_axis=0, concat_axis=0, tiled=True)  26.1 us
    pallas_call x2, Pallas kernels, lines_in(): pl.pallas_call(functools.partial(lines_in_kernel, plan, parity), grid=(sl...  25.5 us
    all_to_all x3, starting transfers between devices, across(): lax.all_to_all(lines, ('col', 'row'), split_axis=0, concat_axis=0, tiled=...  25.1 us
  transfers between devices with their start and end apart: 15, of which 9 were waited for; matrix products, arithmetic and copies ran while one was open for 7% of the time, Pallas kernels for 14%

profile of v1, /device:TPU:9, one launch (start us, length us, event | category | flops | bytes accessed | tf_op | source)
XLA Modules:
  0.0 883.3 jit_solution(4486094038555070418)
XLA Ops:
  5.7 5.6 collective-permute-done.got
  14.7 7.9 pack.1
  35.7 75.5 %collective-permute-done.2 = f32[4,2,40,1408]{3,2,1,0:T(8,128)S(1)} collective-permute-done((f32[4,2,40,1408]{3,2,1,0:T(8,128)}, f32[4,2,40,1408]{3,2,1,0:T(8,128)S(1)}, u32[]{:S(2)}, u32[]{:S(2)}) %collective-permute-start.2) | collective-permute-done | bytes 1802272 | tf_op jit(solution)/shard_map/ppermute | solution.py:814
  116.9 21.5 %all-to-all-done.2.mv2 = f32[4,2,40,1408]{3,2,1,0:T(8,128)S(1)} async-done(((f32[4,2,40,1408]{3,2,1,0:T(8,128)}), f32[4,2,40,1408]{3,2,1,0:T(8,128)S(1)}, u32[]{:S(2)}, u32[]{:S(2)}) %all-to-all-start.2) | async-done | bytes 1802272 | tf_op jit(solution)/shard_map/all_to_all | solution.py:807
  146.4 19.0 %all-to-all-done.1.mv1 = f32[4,2,40,1408]{3,2,1,0:T(8,128)} async-done(((f32[4,2,40,1408]{3,2,1,0:T(8,128)}), f32[4,2,40,1408]{3,2,1,0:T(8,128)}, u32[]{:S(2)}, u32[]{:S(2)}) %all-to-all-start.1) | async-done | bytes 1802272 | tf_op jit(solution)/shard_map/all_to_all | solution.py:807
  165.4 12.6 %lines_in.2 = f32[32,2,2,88,128]{4,3,2,1,0:T(8,128)} custom-call(s32[13]{0:T(128)S(1)} %fusion.115.info, f32[4,2,88,1408]{3,2,1,0:T(8,128)} %all-to-all-done.own, f32[4,2,40,1408]{3,2,1,0:T(8,128)} %all-to-all-done.1.mv1, f32[4,2,40,1408]{3,2,1,0:T(8,128)S(1)} %all-to-all-done.2.mv2, f32[32,2,128]{2,1,0:T(2,128)S(1)} %get-tuple-element.34.turn, ...), custom_call_target="tpu_custom_call" | custom-call | flops 4294967296 | bytes 16777216 | tf_op jit(solution)/shard_map/lines_in/pallas_call | solution.py:423
  178.0 6.4 all-to-all-start.3
  184.4 13.0 %lines_in.3 = f32[32,2,2,88,128]{4,3,2,1,0:T(8,128)} custom-call(s32[13]{0:T(128)S(1)} %fusion.115.info, f32[4,2,88,1408]{3,2,1,0:T(8,128)} %all-to-all-done.own, f32[4,2,40,1408]{3,2,1,0:T(8,128)} %all-to-all-done.1.mv1, f32[4,2,40,1408]{3,2,1,0:T(8,128)S(1)} %all-to-all-done.2.mv2, f32[32,2,128]{2,1,0:T(2,128)S(1)} %get-tuple-element.33.turn, ...), custom_call_target="tpu_custom_call" | custom-call | flops 4294967296 | bytes 16777216 | tf_op jit(solution)/shard_map/lines_in/pallas_call | solution.py:423
  197.4 111.9 %all-to-all-done.3.src = f32[32,2,2,88,128]{4,3,2,1,0:T(8,128)} async-done(((f32[32,2,2,88,128]{4,3,2,1,0:T(8,128)}), f32[32,2,2,88,128]{4,3,2,1,0:T(8,128)}, u32[]{:S(2)}, u32[]{:S(2)}) %all-to-all-start.3) | async-done | bytes 5767200 | tf_op jit(solution)/shard_map/all_to_all | solution.py:810
  309.2 9.3 %all-to-all-start.5 = ((f32[32,2,2,88,128]{4,3,2,1,0:T(8,128)}), f32[32,2,2,88,128]{4,3,2,1,0:T(8,128)}, u32[]{:S(2)}, u32[]{:S(2)}) async-start(f32[32,2,2,88,128]{4,3,2,1,0:T(8,128)} %lines_in.3), calls=%async_computation.5 | async-start | bytes 11534336 | tf_op jit(solution)/shard_map/all_to_all | solution.py:810
  331.0 57.2 %columns.2 = f32[32,2,2,88,128]{4,3,2,1,0:T(8,128)} custom-call(f32[32,2,2,88,128]{4,3,2,1,0:T(8,128)} %all-to-all-done.3.src, bf16[64,128,256]{2,1,0:T(8,128)(2,1)} %get-tuple-element.22.th, bf16[64,128,256]{2,1,0:T(8,128)(2,1)} %get-tuple-element.21.tl, bf16[64,256,128]{2,1,0:T(8,128)(2,1)} %get-tuple-element.20.fh, bf16[64,256,128]{2,1,0:T(8,128)(2,1)} %get-tuple-element.19.fl), custom_call_target="tpu_custom_call" | custom-call | flops 17179869184 | bytes 31457280 | tf_op jit(solution)/shard_map/columns/pallas_call | solution.py:509
  388.2 55.2 %all-to-all-done.5.src = f32[32,2,2,88,128]{4,3,2,1,0:T(8,128)} async-done(((f32[32,2,2,88,128]{4,3,2,1,0:T(8,128)}), f32[32,2,2,88,128]{4,3,2,1,0:T(8,128)}, u32[]{:S(2)}, u32[]{:S(2)}) %all-to-all-start.5) | async-done | bytes 5767200 | tf_op jit(solution)/shard_map/all_to_all | solution.py:810
  443.4 9.3 %all-to-all-start.4 = ((f32[32,2,2,88,128]{4,3,2,1,0:T(8,128)}), f32[32,2,2,88,128]{4,3,2,1,0:T(8,128)}, u32[]{:S(2)}, u32[]{:S(2)}) async-start(f32[32,2,2,88,128]{4,3,2,1,0:T(8,128)} %columns.2), calls=%async_computation.4 | async-start | bytes 11534336 | tf_op jit(solution)/shard_map/all_to_all | solution.py:810
  452.8 57.1 %columns.3 = f32[32,2,2,88,128]{4,3,2,1,0:T(8,128)} custom-call(f32[32,2,2,88,128]{4,3,2,1,0:T(8,128)} %all-to-all-done.5.src, bf16[64,128,256]{2,1,0:T(8,128)(2,1)} %get-tuple-element.22.th, bf16[64,128,256]{2,1,0:T(8,128)(2,1)} %get-tuple-element.21.tl, bf16[64,256,128]{2,1,0:T(8,128)(2,1)} %get-tuple-element.20.fh, bf16[64,256,128]{2,1,0:T(8,128)(2,1)} %get-tuple-element.19.fl), custom_call_target="tpu_custom_call" | custom-call | flops 17179869184 | bytes 31457280 | tf_op jit(solution)/shard_map/columns/pallas_call | solution.py:509
  509.9 67.7 %all-to-all-done.4.got0 = f32[32,2,2,88,128]{4,3,2,1,0:T(8,128)} async-done(((f32[32,2,2,88,128]{4,3,2,1,0:T(8,128)}), f32[32,2,2,88,128]{4,3,2,1,0:T(8,128)}, u32[]{:S(2)}, u32[]{:S(2)}) %all-to-all-start.4) | async-done | bytes 5767200 | tf_op jit(solution)/shard_map/all_to_all | solution.py:810
  577.6 136.0 %all_to_all.50.got1 = f32[32,2,2,88,128]{4,3,2,1,0:T(8,128)} all-to-all(f32[32,2,2,88,128]{4,3,2,1,0:T(8,128)} %columns.3), channel_id=1, replica_groups=mesh['row'=4,'col'=8] {'col','row'}, dimensions={0} | all-to-all | bytes 11534336 | tf_op jit(solution)/shard_map/all_to_all | solution.py:810
  713.6 15.8 %lines_out.1 = (f32[4,2,88,1408]{3,2,1,0:T(8,128)}, f32[4,2,40,1408]{3,2,1,0:T(8,128)}, f32[4,2,40,1408]{3,2,1,0:T(8,128)S(1)}) custom-call(s32[13]{0:T(128)S(1)} %fusion.115.info, f32[32,2,2,88,128]{4,3,2,1,0:T(8,128)} %all-to-all-done.4.got0, f32[32,2,2,88,128]{4,3,2,1,0:T(8,128)} %all_to_all.50.got1, f32[2,32,2,128]{3,2,1,0:T(2,128)S(1)} %maximum_bitcast_fusion.turn, ...), custom_call_target="tpu_custom_call" | custom-call | flops 8589934592 | bytes 23068672 | tf_op jit(solution)/shard_map/lines_out/pallas_call | solution.py:577
  729.4 26.1 %all_to_all.51 = f32[4,2,40,1408]{3,2,1,0:T(8,128)} all-to-all(f32[4,2,40,1408]{3,2,1,0:T(8,128)S(1)} %get-tuple-element.16), channel_id=1, replica_groups=mesh['row'=4,'col'=8] {'row'}, dimensions={0} | all-to-all | bytes 3604480 | tf_op jit(solution)/shard_map/all_to_all | solution.py:807
  761.3 20.3 %all-to-all-done.8 = f32[4,2,40,1408]{3,2,1,0:T(8,128)S(1)} async-done(((f32[4,2,40,1408]{3,2,1,0:T(8,128)}), f32[4,2,40,1408]{3,2,1,0:T(8,128)S(1)}, u32[]{:S(2)}, u32[]{:S(2)}) %all-to-all-start.8) | async-done | bytes 1802272 | tf_op jit(solution)/shard_map/all_to_all | solution.py:807
  781.6 5.6 all-to-all-start.7
  789.1 23.9 %multiply_subtract_fusion.2 = (f32[512,2048]{1,0:T(8,128)}, f32[512,2048]{1,0:T(8,128)}, f32[512,2048]{1,0:T(8,128)}, f32[512,2048]{1,0:T(8,128)}) fusion(f32[512]{0:T(512)S(1)} %multiply_multiply_fusion.2, s32[2048]{0:T(1024)S(1)} %get-tuple-element.48, s32[2048]{0:T(1024)S(1)} %get-tuple-element.47, pred[2048]{0:T(1024)(128)(4,1)S(1)} %fusion.113, ...), kind=kLoop, calls=%fused_computation.105 | loop fusion | flops 102760448 | bytes 16799744 | tf_op jit(solution)/shard_map/sub | solution.py:46
  813.0 19.0 %all-to-all-done.7.own = f32[4,2,88,1408]{3,2,1,0:T(8,128)} async-done(((f32[4,2,88,1408]{3,2,1,0:T(8,128)}), f32[4,2,88,1408]{3,2,1,0:T(8,128)}, u32[]{:S(2)}, u32[]{:S(2)}) %all-to-all-start.7) | async-done | bytes 3964960 | tf_op jit(solution)/shard_map/all_to_all | solution.py:807
  843.5 21.0 %multiply_add_fusion = f32[1,2,512,2048]{3,2,1,0:T(8,128)} fusion(f32[1,2,512,2048]{3,2,1,0:T(8,128)} %param.9, f32[1,2,512,2048]{3,2,1,0:T(8,128)} %param.10, f32[1,2,512,2048]{3,2,1,0:T(8,128)} %param.8, f32[1,2,512,2048]{3,2,1,0:T(8,128)} %param.6, f32[512,2048]{1,0:T(8,128)} %get-tuple-element.38, f32[512,2048]{1,0:T(8,128)} %get-tuple-element.39, ...), kind=kLoop, calls=%fused_computation.8 | loop fusion | flops 12582912 | bytes 54525952 | tf_op jit(solution)/shard_map/add | solution.py:849
  870.0 13.3 %unpack.1 = f32[2,512,2048]{2,1,0:T(8,128)} custom-call(s32[2]{0:T(128)S(1)} %pad_add_fusion.info, f32[4,2,88,1408]{3,2,1,0:T(8,128)} %all-to-all-done.7.own, f32[4,2,40,1408]{3,2,1,0:T(8,128)S(1)} %add.475.mv, f32[4,2,88,640]{3,2,1,0:T(8,128)} %collective-permute-done.5.got_own, f32[4,2,40,640]{3,2,1,0:T(8,128)S(1)} %collective-permute-done.6.got_mv, ...), custom_call_target="tpu_custom_call" | custom-call | flops 16777216 | bytes 35651584 | tf_op jit(solution)/shard_map/unpack/pallas_call | solution.py:722
  (49 shorter events, 72.8 us)
Async XLA Ops:
  4.3 7.0 collective-permute-start
  11.3 3.4 copy-start.1
  22.6 1.9 copy-start.3
  24.5 87.9 %all-to-all-start = ((f32[4,2,88,1408]{3,2,1,0:T(8,128)}), f32[4,2,88,1408]{3,2,1,0:T(8,128)}, u32[]{:S(2)}, u32[]{:S(2)}) async-start(f32[4,2,88,1408]{3,2,1,0:T(8,128)} %copy-done.3), calls=%async_computation | async-start | bytes 7929856 | tf_op jit(solution)/shard_map/all_to_all | solution.py:807
  29.4 81.7 %collective-permute-start.2 = (f32[4,2,40,1408]{3,2,1,0:T(8,128)}, f32[4,2,40,1408]{3,2,1,0:T(8,128)S(1)}, u32[]{:S(2)}, u32[]{:S(2)}) collective-permute-start(f32[4,2,40,1408]{3,2,1,0:T(8,128)} %get-tuple-element.13), channel_id=1, source_target_pairs={{2,6},{3,7},{10,14},{11,15},{18,22},{19,23},{26,30},{27,31}} | collective-permute-start | bytes 5406728 | tf_op jit(solution)/shard_map/ppermute | solution.py:814
  33.8 83.1 %collective-permute-start.1 = (f32[4,2,40,1408]{3,2,1,0:T(8,128)}, f32[4,2,40,1408]{3,2,1,0:T(8,128)}, u32[]{:S(2)}, u32[]{:S(2)}) collective-permute-start(f32[4,2,40,1408]{3,2,1,0:T(8,128)} %get-tuple-element.13), channel_id=1, source_target_pairs={{4,5},{0,6},{1,7},{12,13},{8,14},{9,15},{20,21},{16,22},{17,23},{2... | collective-permute-start | bytes 5406728 | tf_op jit(solution)/shard_map/ppermute | solution.py:813
  111.2 1.3 copy-start.4
  112.4 26.0 %all-to-all-start.2 = ((f32[4,2,40,1408]{3,2,1,0:T(8,128)}), f32[4,2,40,1408]{3,2,1,0:T(8,128)S(1)}, u32[]{:S(2)}, u32[]{:S(2)}) async-start(f32[4,2,40,1408]{3,2,1,0:T(8,128)} %copy-done.4), calls=%async_computation.2 | async-start | bytes 3604480 | tf_op jit(solution)/shard_map/all_to_all | solution.py:807
  138.4 27.0 %all-to-all-start.1 = ((f32[4,2,40,1408]{3,2,1,0:T(8,128)}), f32[4,2,40,1408]{3,2,1,0:T(8,128)}, u32[]{:S(2)}, u32[]{:S(2)}) async-start(f32[4,2,40,1408]{3,2,1,0:T(8,128)} %collective-permute-done.1), calls=%async_computation.1 | async-start | bytes 3604480 | tf_op jit(solution)/shard_map/all_to_all | solution.py:807
  178.0 131.2 %all-to-all-start.3 = ((f32[32,2,2,88,128]{4,3,2,1,0:T(8,128)}), f32[32,2,2,88,128]{4,3,2,1,0:T(8,128)}, u32[]{:S(2)}, u32[]{:S(2)}) async-start(f32[32,2,2,88,128]{4,3,2,1,0:T(8,128)} %lines_in.2), calls=%async_computation.3 | async-start | bytes 11534336 | tf_op jit(solution)/shard_map/all_to_all | solution.py:810
  309.2 134.2 %all-to-all-start.5 = ((f32[32,2,2,88,128]{4,3,2,1,0:T(8,128)}), f32[32,2,2,88,128]{4,3,2,1,0:T(8,128)}, u32[]{:S(2)}, u32[]{:S(2)}) async-start(f32[32,2,2,88,128]{4,3,2,1,0:T(8,128)} %lines_in.3), calls=%async_computation.5 | async-start | bytes 11534336 | tf_op jit(solution)/shard_map/all_to_all | solution.py:810
  443.4 134.2 %all-to-all-start.4 = ((f32[32,2,2,88,128]{4,3,2,1,0:T(8,128)}), f32[32,2,2,88,128]{4,3,2,1,0:T(8,128)}, u32[]{:S(2)}, u32[]{:S(2)}) async-start(f32[32,2,2,88,128]{4,3,2,1,0:T(8,128)} %columns.2), calls=%async_computation.4 | async-start | bytes 11534336 | tf_op jit(solution)/shard_map/all_to_all | solution.py:810
  755.5 26.1 %all-to-all-start.8 = ((f32[4,2,40,1408]{3,2,1,0:T(8,128)}), f32[4,2,40,1408]{3,2,1,0:T(8,128)S(1)}, u32[]{:S(2)}, u32[]{:S(2)}) async-start(f32[4,2,40,1408]{3,2,1,0:T(8,128)} %get-tuple-element.15), calls=%async_computation.8 | async-start | bytes 3604480 | tf_op jit(solution)/shard_map/all_to_all | solution.py:807
  760.0 79.8 %collective-permute-start.4 = (f32[4,2,40,1408]{3,2,1,0:T(8,128)}, f32[4,2,40,1408]{3,2,1,0:T(8,128)}, u32[]{:S(2)}, u32[]{:S(2)}) collective-permute-start(f32[4,2,40,1408]{3,2,1,0:T(8,128)} %all_to_all.51), channel_id=1, source_target_pairs={{6,2},{7,3},{14,10},{15,11},{22,18},{23,19},{30,26},{31,27}} | collective-permute-start | bytes 5406728 | tf_op jit(solution)/shard_map/ppermute | solution.py:831
  781.6 50.4 %all-to-all-start.7 = ((f32[4,2,88,1408]{3,2,1,0:T(8,128)}), f32[4,2,88,1408]{3,2,1,0:T(8,128)}, u32[]{:S(2)}, u32[]{:S(2)}) async-start(f32[4,2,88,1408]{3,2,1,0:T(8,128)} %get-tuple-element.14), calls=%async_computation.7 | async-start | bytes 7929856 | tf_op jit(solution)/shard_map/all_to_all | solution.py:807
  787.3 52.6 %collective-permute-start.3 = (f32[4,2,40,1408]{3,2,1,0:T(8,128)S(1)}, f32[4,2,40,1408]{3,2,1,0:T(8,128)}, u32[]{:S(2)}, u32[]{:S(2)}) collective-permute-start(f32[4,2,40,1408]{3,2,1,0:T(8,128)S(1)} %all-to-all-done.8), channel_id=1, source_target_pairs={{5,4},{6,0},{7,1},{13,12},{14,8},{15,9},{21,20},{22,16},{23,17},{2... | collective-permute-start | bytes 5406728 | tf_op jit(solution)/shard_map/ppermute | solution.py:831
  835.6 28.8 %collective-permute-start.5 = (f32[4,2,88,640]{3,2,1,0:T(8,128)}, f32[4,2,88,640]{3,2,1,0:T(8,128)}, u32[]{:S(2)}, u32[]{:S(2)}) collective-permute-start(f32[4,2,88,640]{3,2,1,0:T(8,128)} %slice_select_fusion), channel_id=1, source_target_pairs={{8,0},{16,24},{9,1},{17,25},{10,2},{18,26},{11,3},{19,27},{12,4},{... | collective-permute-start | bytes 5406728 | tf_op jit(solution)/shard_map/ppermute | solution.py:835
  842.1 22.3 %collective-permute-start.6 = (f32[4,2,40,640]{3,2,1,0:T(8,128)S(1)}, f32[4,2,40,640]{3,2,1,0:T(8,128)S(1)}, u32[]{:S(2)}, u32[]{:S(2)}) collective-permute-start(f32[4,2,40,640]{3,2,1,0:T(8,128)S(1)} %slice_select_fusion.1), channel_id=1, source_target_pairs={{8,0},{16,24},{9,1},{17,25},{10,2},{18,26},{11,3},{19,27},{12,4},{... | collective-permute-start | bytes 2457608 | tf_op jit(solution)/shard_map/ppermute | solution.py:835
  864.5 3.4 copy-start
  867.8 2.2 copy-start.2

commit v2 on v1

--- a/solution.py
+++ b/solution.py
@@ -228,13 +228,11 @@
     high = HALF - (length - kept + 1) // LANES
     if low != high or low % 2 or low > HALF // 2:
         return None
-    per = low // 2
-    home_tiles = block_y // LANES
-    if not per < home_tiles < low:
+    if not block_y < low * LANES < 2 * block_y or block_y % LANES:
         return None
     return dict(
         kept=kept, stride=stride, groups=groups, own=own, slots=slots, extra=extra,
-        moves=moves, low=low, per=per, home=home_tiles, rows=rows, cols=cols,
+        moves=moves, low=low, rows=rows, cols=cols,
         block_x=block_x, block_y=block_y, length=length,
     )
 
@@ -259,14 +257,12 @@
     slots, extra = plan["slots"], plan["extra"]
     for col in range(plan["cols"]):
         base = [col * plan["block_x"] + slot * plan["stride"] for slot in range(slots)]
-        flags = [0, 0]
         for donor, taker, turn in plan["moves"]:
             if taker == col:
-                flags[turn] = 1
                 start = slots - extra if turn == 0 else 0
                 for step in range(extra):
                     base[start + step] = donor * plan["block_x"] + (slots + step) * plan["stride"]
-        rows.append(base + flags)
+        rows.append(base)
     return rows
 
 
@@ -345,8 +341,7 @@
 
 def tile_of(plan, a):
     low = plan["low"]
-    t = a if a < low else a - (HALF - 2 * low)
-    return t // plan["per"], (t % plan["per"]) * LANES
+    return LANES * (a if a < low else a - (HALF - 2 * low))
 
 
 def kept_tiles(plan):
@@ -366,11 +361,9 @@
     return (3 * wave_x < plan["length"]) & (3 * jnp.abs(wave_y) < plan["length"])
 
 
-def lines_in_kernel(plan, parity, info, own, mv1, mv2, turn, wh, wl, out, scr):
-    slots, extra, length = plan["slots"], plan["extra"], plan["length"]
+def lines_in_kernel(plan, parity, info, lines, turn, wh, wl, out, scr):
+    length = plan["length"]
     j = pl.program_id(0)
-    use1 = (info[slots] == 1) & (j >= slots - extra)
-    use2 = (info[slots + 1] == 1) & (j < extra)
     wave_x = info[j] + sublane_iota()
     kx = wave_x.astype(jnp.float32)
     doubled = jnp.where(wave_x == 0, 1.0, 2.0) * (length / 9.0)
@@ -379,19 +372,18 @@
     for field in range(2):
         tiles = {}
         for a in kept_tiles(plan):
-            r, off = tile_of(plan, a)
+            off = tile_of(plan, a)
             wave_y = lane + (LANES * a - (length if a >= HALF // 2 else 0))
             square = (wave_x * wave_x + wave_y * wave_y)
-            value = doubled / jnp.maximum(square, 1).astype(jnp.float32)
-            factor = jnp.where(keep_of(plan, wave_x, wave_y), value, 0.0)
+            factor = doubled / jnp.maximum(square, 1).astype(jnp.float32)
+            keep = keep_of(plan, wave_x, wave_y)
             if field == 0:
                 factor = factor * (step * wave_y.astype(jnp.float32))
             else:
                 factor = factor * (-step * kx)
             parts = []
             for p in range(2):
-                at = (r, p, slice(None), slice(off, off + LANES))
-                parts.append(jnp.where(use1, mv1[at], jnp.where(use2, mv2[at], own[at])))
+                parts.append(jnp.where(keep, lines[p, 0, :, off:off + LANES], 0.0))
             tiles[a] = (-factor * parts[1], factor * parts[0])
         mixed = []
         for a in range(HALF // 2):
@@ -414,20 +406,17 @@
             )
 
 
-def lines_in(plan, parity, info, own, mv1, mv2, turn, table):
-    slots, extra, rows = plan["slots"], plan["extra"], plan["rows"]
-    width = plan["per"] * LANES
-    block = (rows, 2, SUBL, width)
-    devices = rows * plan["cols"]
+def lines_in(plan, parity, info, lines, turn, table):
+    slots = plan["slots"]
+    width = 2 * plan["low"] * LANES
+    devices = plan["rows"] * plan["cols"]
     whole = lambda shape: pl.BlockSpec(shape, lambda j: (0,) * len(shape))
     return pl.pallas_call(
         functools.partial(lines_in_kernel, plan, parity),
         grid=(slots,),
         in_specs=[
             pl.BlockSpec(memory_space=pltpu.SMEM),
-            pl.BlockSpec(block, lambda j: (0, 0, j, 0)),
-            pl.BlockSpec(block, lambda j: (0, 0, jnp.maximum(j - (slots - extra), 0), 0)),
-            pl.BlockSpec(block, lambda j: (0, 0, jnp.minimum(j, extra - 1), 0)),
+            pl.BlockSpec((2, 1, SUBL, width), lambda j: (0, j, 0, 0)),
             whole((HALF // 2, 2, LANES)),
             whole((2 * LANES, 2 * LANES)),
             whole((2 * LANES, 2 * LANES)),
@@ -435,10 +424,10 @@
         out_specs=pl.BlockSpec((devices, 2, 2, SUBL, LANES), lambda j: (0, 0, 0, j, 0)),
         out_shape=jax.ShapeDtypeStruct((devices, 2, 2, slots * SUBL, LANES), jnp.float32),
         scratch_shapes=[pltpu.VMEM((HALF // 2 * SUBL, 2 * LANES), jnp.float32)],
-        compiler_params=pltpu.CompilerParams(vmem_limit_bytes=50 << 20),
+        compiler_params=pltpu.CompilerParams(vmem_limit_bytes=60 << 20),
         cost_estimate=pl.CostEstimate(flops=4 << 30, bytes_accessed=16 << 20, transcendentals=0),
         name="lines_in",
-    )(info, own, mv1, mv2, turn, *table)
+    )(info, lines, turn, *table)
 
 
 def columns_kernel(plan, src, th, tl, fh, fl, out, mid):
@@ -518,8 +507,8 @@
     )(spread, *tables)
 
 
-def lines_out_kernel(plan, info, got0, got1, turn, wh, wl, own, mv1, mv2, scr, acc):
-    slots, extra, length = plan["slots"], plan["extra"], plan["length"]
+def lines_out_kernel(plan, info, got0, got1, turn, wh, wl, lines, scr, acc):
+    length = plan["length"]
     j = pl.program_id(0)
     wave_x = info[j] + sublane_iota()
     step = wave_scale / length
@@ -549,31 +538,21 @@
                 weight = (kappa_x * kappa_x - kappa_y * kappa_y) * (1.0 / length)
             else:
                 weight = kappa_x * kappa_y * (1.0 / length)
-            r, off = tile_of(plan, a)
+            off = tile_of(plan, a)
             for p in range(2):
                 value = jnp.where(keep, weight * result[a][p], 0.0)
                 if field == 0:
                     acc[t, p] = value
                 else:
-                    own[r, p, :, off:off + LANES] = acc[t, p] + value
-
-    @pl.when(j < extra)
-    def _():
-        mv2[...] = own[...]
-
-    @pl.when(j >= slots - extra)
-    def _():
-        mv1[...] = own[...]
+                    lines[p, 0, :, off:off + LANES] = acc[t, p] + value
 
 
 def lines_out(plan, info, got0, got1, turn, table):
-    slots, extra, rows = plan["slots"], plan["extra"], plan["rows"]
-    width = plan["per"] * LANES
-    block = (rows, 2, SUBL, width)
-    devices = rows * plan["cols"]
+    slots = plan["slots"]
+    width = 2 * plan["low"] * LANES
+    devices = plan["rows"] * plan["cols"]
     whole = lambda shape: pl.BlockSpec(shape, lambda j: (0,) * len(shape))
     got_spec = pl.BlockSpec((devices, 2, 2, SUBL, LANES), lambda j: (0, 0, 0, j, 0))
-    lines = lambda n: jax.ShapeDtypeStruct((rows, 2, n * SUBL, width), jnp.float32)
     return pl.pallas_call(
         functools.partial(lines_out_kernel, plan),
         grid=(slots,),
@@ -585,159 +564,171 @@
             whole((2 * LANES, 2 * LANES)),
             whole((2 * LANES, 2 * LANES)),
         ],
-        out_specs=[
-            pl.BlockSpec(block, lambda j: (0, 0, j, 0)),
-            pl.BlockSpec(block, lambda j: (0, 0, jnp.maximum(j - (slots - extra), 0), 0)),
-            pl.BlockSpec(block, lambda j: (0, 0, jnp.minimum(j, extra - 1), 0)),
-        ],
-        out_shape=[lines(slots), lines(extra), lines(extra)],
+        out_specs=pl.BlockSpec((2, 1, SUBL, width), lambda j: (0, j, 0, 0)),
+        out_shape=jax.ShapeDtypeStruct((2, slots, SUBL, width), jnp.float32),
         scratch_shapes=[
             pltpu.VMEM((2, HALF // 2 * SUBL, 2 * LANES), jnp.float32),
-            pltpu.VMEM((4 * plan["per"], 2, SUBL, LANES), jnp.float32),
+            pltpu.VMEM((2 * plan["low"], 2, SUBL, LANES), jnp.float32),
         ],
-        compiler_params=pltpu.CompilerParams(vmem_limit_bytes=50 << 20),
+        compiler_params=pltpu.CompilerParams(vmem_limit_bytes=60 << 20),
         cost_estimate=pl.CostEstimate(flops=8 << 30, bytes_accessed=22 << 20, transcendentals=0),
         name="lines_out",
     )(info, got0, got1, turn, *table)
 
 
-def pack_kernel(plan, info, field, got, own, mv):
-    per, home, slots, rows = plan["per"], plan["home"], plan["slots"], plan["rows"]
-    j = pl.program_id(0)
-    more = home - per
-    width, full = per * LANES, home * LANES
-    less = width - more * LANES
-
-    def put(dest):
-        for p in range(2):
-            for r in range(rows):
-                at = slice(r * SUBL, (r + 1) * SUBL)
-
-                @pl.when(info[0] == 0)
-                def _():
-                    dest[r, p] = field[0, p, at, :width]
-
-                @pl.when(info[0] == 1)
-                def _():
-                    dest[r, p, :, :more * LANES] = got[p, at, :]
-                    dest[r, p, :, more * LANES:] = field[0, p, at, :less]
-
-                @pl.when(info[0] == 2)
-                def _():
-                    dest[r, p, :, :less] = field[0, p, at, full - less:]
-                    dest[r, p, :, less:] = got[p, at, :]
-
-                @pl.when(info[0] == 3)
-                def _():
-                    dest[r, p] = field[0, p, at, full - width:]
-
-    @pl.when(j < slots)
-    def _():
-        put(own)
-
-    @pl.when(j >= slots)
-    def _():
-        put(mv)
-
-
-def pack(plan, where, field, member, got):
-    slots, extra, rows, groups = plan["slots"], plan["extra"], plan["rows"], plan["groups"]
-    width = plan["per"] * LANES
-    more = (plan["home"] - plan["per"]) * LANES
-    block = (rows, 2, SUBL, width)
-    lines = lambda n: jax.ShapeDtypeStruct((rows, 2, n * SUBL, width), jnp.float32)
+def spans(plan, row):
+    full = plan["block_y"]
+    short = plan["low"] * LANES - full
+    side, inner = row // 2, row % 2
+
+    def at(offset):
+        return pl.multiple_of(offset, LANES)
+
+    return (
+        (at(side * (full - short)), at(side * (full + short) + inner * full), short),
+        (at((1 - side) * short), at(short + side * (full + short)), full - short),
+    )
+
+
+def both_of(row):
+    return row // 2 == row % 2
+
+
+def own_cases(plan):
+    cases = []
+    for col, count in enumerate(plan["own"]):
+        count = min(count, plan["slots"])
+        if not count:
+            continue
+        if cases and cases[-1][2] == count:
+            cases[-1] = (cases[-1][0], col, count)
+        else:
+            cases.append((col, col, count))
+    return cases
+
+
+def exchange_kernel(plan, back, source, target, send, recv):
+    rows, slots, extra = plan["rows"], plan["slots"], plan["extra"]
+    row, col = lax.axis_index("row"), lax.axis_index("col")
+
+    def views(home, lines, begin, count, start, line_row, home_row, piece):
+        home_at, line_at, width = spans(plan, home_row)[piece]
+        return (
+            home.at[:, pl.ds(begin, count), line_row, :, pl.ds(home_at, width)],
+            lines.at[:, pl.ds(start, count), :, pl.ds(line_at, width)],
+        )
+
+    def copy(kind, step, piece, begin, count, start, where, line_row, home_row, turn):
+        if back:
+            dst, src = views(target, source, begin, count, start, line_row, home_row, piece)
+        else:
+            src, dst = views(source, target, begin, count, start, line_row, home_row, piece)
+        if where is None:
+            return pltpu.make_async_copy(src, dst, send.at[kind, step, piece])
+        return pltpu.make_async_remote_copy(
+            src_ref=src, dst_ref=dst, send_sem=send.at[kind + turn, step, piece],
+            recv_sem=recv.at[kind + turn, step, piece], device_id=where,
+            device_id_type=pl.DeviceIdType.MESH,
+        )
+
+    def each(home_row, act):
+        act(0)
+
+        @pl.when(both_of(home_row))
+        def _():
+            act(1)
+
+    def moved(verb):
+        for donor, taker, turn in plan["moves"]:
+            start = slots - extra if turn == 0 else 0
+            sender, receiver = (taker, donor) if back else (donor, taker)
+            peer = sender if verb == "recv" else receiver
+
+            @pl.when(col == (receiver if verb == "recv" else sender))
+            def _():
+                for step in range(rows):
+                    other = (row + step) % rows if verb != "recv" else (row + rows - step) % rows
+                    mine_is_line = back == (verb != "recv")
+                    line_row, home_row = (row, other) if mine_is_line else (other, row)
+
+                    def act(piece):
+                        it = copy(
+                            1, step, piece, slots, extra, start,
+                            {"col": peer, "row": other}, line_row, home_row, turn,
+                        )
+                        do(it, verb)
+
+                    each(home_row, act)
+
+    def do(it, verb):
+        if verb == "start":
+            it.start()
+        elif verb == "send":
+            it.wait_send()
+        else:
+            it.wait_recv()
+
+    def owned(verb):
+        for first, last, count in own_cases(plan):
+            @pl.when((col >= first) & (col <= last))
+            def _():
+                for step in range(1, rows):
+                    other = (row + step) % rows if verb != "recv" else (row + rows - step) % rows
+                    mine_is_line = back == (verb != "recv")
+                    line_row, home_row = (row, other) if mine_is_line else (other, row)
+
+                    def act(piece):
+                        do(
+                            copy(
+                                0, step, piece, 0, count, 0, {"row": other}, line_row,
+                                home_row, 0,
+                            ),
+                            verb,
+                        )
+
+                    each(home_row, act)
+
+    def local(verb):
+        for first, last, count in own_cases(plan):
+            @pl.when((col >= first) & (col <= last))
+            def _():
+                def act(piece):
+                    it = copy(0, 0, piece, 0, count, 0, None, row, row, 0)
+                    if verb == "start":
+                        it.start()
+                    else:
+                        it.wait()
+
+                each(row, act)
+
+    moved("start")
+    owned("start")
+    local("start")
+    local("wait")
+    owned("recv")
+    moved("recv")
+    owned("send")
+    moved("send")
+
+
+def exchange(plan, back, source):
+    rows, groups = plan["rows"], plan["groups"]
+    home = (2, groups, rows, SUBL, plan["block_y"])
+    lines = (2, plan["slots"], SUBL, 2 * plan["low"] * LANES)
+    turns_used = 3
     return pl.pallas_call(
-        functools.partial(pack_kernel, plan),
-        grid=(groups,),
-        in_specs=[
-            pl.BlockSpec(memory_space=pltpu.SMEM),
-            pl.BlockSpec((1, 2, plan["stride"], plan["block_y"]), lambda j: (member, 0, j, 0)),
-            pl.BlockSpec((2, plan["stride"], more), lambda j: (0, j, 0)),
+        functools.partial(exchange_kernel, plan, back),
+        in_specs=[pl.BlockSpec(memory_space=pl.ANY)],
+        out_specs=pl.BlockSpec(memory_space=pl.ANY),
+        out_shape=jax.ShapeDtypeStruct(home if back else lines, jnp.float32),
+        scratch_shapes=[
+            pltpu.SemaphoreType.DMA((turns_used, rows, 2)),
+            pltpu.SemaphoreType.DMA((turns_used, rows, 2)),
         ],
-        out_specs=[
-            pl.BlockSpec(block, lambda j: (0, 0, jnp.minimum(j, slots - 1), 0)),
-            pl.BlockSpec(block, lambda j: (0, 0, jnp.maximum(j - slots, 0), 0)),
-        ],
-        out_shape=[lines(slots), lines(extra)],
-        compiler_params=pltpu.CompilerParams(vmem_limit_bytes=32 << 20),
-        cost_estimate=pl.CostEstimate(flops=1 << 24, bytes_accessed=14 << 20, transcendentals=0),
-        name="pack",
-    )(where, field, got)
-
-
-def unpack_kernel(plan, info, own, mv, got_own, got_mv, linear, weight, out, term):
-    per, home, slots, rows = plan["per"], plan["home"], plan["slots"], plan["rows"]
-    j = pl.program_id(0)
-    more = (home - per) * LANES
-    width, full = per * LANES, home * LANES
-    less = width - more
-    keep_x = info[1] + j * plan["stride"]
-
-    def put(lines, got):
-        for p in range(2):
-            for r in range(rows):
-                at = slice(r * SUBL, (r + 1) * SUBL)
-
-                @pl.when(info[0] == 0)
-                def _():
-                    term[p, at, :width] = lines[r, p]
-                    term[p, at, width:] = got[r, p]
-
-                @pl.when(info[0] == 1)
-                def _():
-                    term[p, at, :less] = lines[r, p, :, more:]
-                    term[p, at, less:] = jnp.zeros((SUBL, full - less), jnp.float32)
-
-                @pl.when(info[0] == 2)
-                def _():
-                    term[p, at, full - less:] = lines[r, p, :, :less]
-                    term[p, at, :full - less] = jnp.zeros((SUBL, full - less), jnp.float32)
-
-                @pl.when(info[0] == 3)
-                def _():
-                    term[p, at, full - width:] = lines[r, p]
-                    term[p, at, :full - width] = got[r, p]
-
-    @pl.when(j < slots)
-    def _():
-        put(own, got_own)
-
-    @pl.when(j >= slots)
-    def _():
-        put(mv, got_mv)
-
-    wave_x = keep_x + lax.broadcasted_iota(jnp.int32, (plan["stride"], full), 0)
-    keep = 3 * wave_x < plan["length"]
-    for p in range(2):
-        out[p] = linear[p] + jnp.where(keep, weight[...] * term[p], 0.0)
-
-
-def unpack(plan, where, own, mv, got_own, got_mv, linear, weight):
-    slots, rows, groups = plan["slots"], plan["rows"], plan["groups"]
-    width = plan["per"] * LANES
-    more = (plan["home"] - plan["per"]) * LANES
-    own_at = lambda j: (0, 0, jnp.minimum(j, slots - 1), 0)
-    mv_at = lambda j: (0, 0, jnp.maximum(j - slots, 0), 0)
-    rowed = pl.BlockSpec((2, plan["stride"], plan["block_y"]), lambda j: (0, j, 0))
-    return pl.pallas_call(
-        functools.partial(unpack_kernel, plan),
-        grid=(groups,),
-        in_specs=[
-            pl.BlockSpec(memory_space=pltpu.SMEM),
-            pl.BlockSpec((rows, 2, SUBL, width), own_at),
-            pl.BlockSpec((rows, 2, SUBL, width), mv_at),
-            pl.BlockSpec((rows, 2, SUBL, more), own_at),
-            pl.BlockSpec((rows, 2, SUBL, more), mv_at),
-            rowed,
-            pl.BlockSpec((plan["stride"], plan["block_y"]), lambda j: (j, 0)),
-        ],
-        out_specs=rowed,
-        out_shape=jax.ShapeDtypeStruct(linear.shape, jnp.float32),
-        scratch_shapes=[pltpu.VMEM((2, plan["stride"], plan["block_y"]), jnp.float32)],
-        compiler_params=pltpu.CompilerParams(vmem_limit_bytes=32 << 20),
-        cost_estimate=pl.CostEstimate(flops=1 << 24, bytes_accessed=34 << 20, transcendentals=0),
-        name="unpack",
-    )(where, own, mv, got_own, got_mv, linear, weight)
+        compiler_params=pltpu.CompilerParams(has_side_effects=True, vmem_limit_bytes=60 << 20),
+        cost_estimate=pl.CostEstimate(flops=1 << 34, bytes_accessed=16 << 20, transcendentals=0),
+        name="lines_home" if back else "home_lines",
+    )(source)
 
 
 def split_table(values):
@@ -787,54 +778,25 @@
     return inverse + forward
 
 
-def fast_term(plan, member, section_field, finish):
-    rows, cols, length = plan["rows"], plan["cols"], plan["length"]
-    slots, per, home = plan["slots"], plan["per"], plan["home"]
-    row = lax.axis_index("row")
-    col = lax.axis_index("col")
-    where = jnp.stack([row, col * plan["block_x"]]).astype(jnp.int32)
-    info = jnp.asarray(line_info(plan), jnp.int32)[col]
-    info = info + jnp.where(jnp.arange(slots + 2) < slots, row * SUBL, 0).astype(jnp.int32)
-    more = (home - per) * LANES
-    edge = jnp.where(
-        row < rows // 2, section_field[member, :, :, per * LANES:],
-        section_field[member, :, :, :more],
-    )
-    got = lax.ppermute(edge, "row", [(0, 1), (3, 2)])
-    own, moved = pack(plan, where, section_field, member, got)
-
-    def swap(lines):
-        return lax.all_to_all(lines, "row", split_axis=0, concat_axis=0, tiled=True)
+def fast_term(plan, field):
+    rows = plan["rows"]
+    row, col = lax.axis_index("row"), lax.axis_index("col")
+    info = jnp.asarray(line_info(plan), jnp.int32)[col] + (row * SUBL).astype(jnp.int32)
 
     def across(lines):
         return lax.all_to_all(lines, ("col", "row"), split_axis=0, concat_axis=0, tiled=True)
 
-    pairs = [[(d, t) for d, t, turn in plan["moves"] if turn == k] for k in range(2)]
-    moved1 = lax.ppermute(moved, "col", pairs[0])
-    moved2 = lax.ppermute(moved, "col", pairs[1])
-    own = swap(own)
-    moved1 = swap(moved1)
-    moved2 = swap(moved2)
-    turn = turns(length)
+    home = field.reshape(2, plan["groups"], rows, SUBL, plan["block_y"])
+    lines = exchange(plan, False, home)
+    turn = turns(plan["length"])
     table = lane_table(1.0)
     spread = [
-        across(lines_in(plan, parity, info, own, moved1, moved2, turn[parity], table))
-        for parity in range(2)
+        across(lines_in(plan, parity, info, lines, turn[parity], table)) for parity in range(2)
     ]
-    tables = column_tables(length)
+    tables = column_tables(plan["length"])
     back = [across(columns(plan, part, tables)) for part in spread]
-    own, moved1, moved2 = lines_out(plan, info, *back, turn, lane_table(-1.0))
-    own = swap(own)
-    moved1 = swap(moved1)
-    moved2 = swap(moved2)
-    flip = [[(t, d) for d, t in group] for group in pairs]
-    moved = lax.ppermute(moved1, "col", flip[0]) + lax.ppermute(moved2, "col", flip[1])
-
-    def edge_of(lines):
-        side = jnp.where(row < rows // 2, lines[..., :more], lines[..., per * LANES - more:])
-        return lax.ppermute(side, "row", [(1, 0), (2, 3)])
-
-    return finish(where, own, moved, edge_of(own), edge_of(moved))
+    lines = lines_out(plan, info, *back, turn, lane_table(-1.0))
+    return exchange(plan, True, lines).reshape(field.shape)
 
 
 def fast_device(plan, start_field, section_field, start_term, first_term, second_term):
@@ -851,15 +813,9 @@
         + 2.0 * weight_b * (first_term + second_term)
     )
     linear, weight_c = lax.optimization_barrier((linear, weight_c))
-    out = []
-    for member in range(start_field.shape[0]):
-        out.append(
-            fast_term(
-                plan, member, section_field,
-                lambda where, *parts: unpack(plan, where, *parts, linear[member], weight_c),
-            )
-        )
-    return jnp.stack(out)
+    term = jnp.stack([fast_term(plan, section_field[m]) for m in range(start_field.shape[0])])
+    keep = keep_of(plan, wave_x, wave_y)
+    return linear + jnp.where(keep, weight_c * term, 0.0)
 
 
 def solution(mesh):

time: 891 us -> 755 us (0.85)
  blocking collectives: 162 us -> 0 us
  Pallas kernels: 177 us -> 312 us
  waiting for transfers between devices: 396 us -> 317 us
  starting transfers between devices: 66.1 us -> 52.6 us
  local copies, waits for them, and re-layouts: 12.1 us -> 0.63 us
    all_to_all x2 -> x0, blocking collectives: 162 us -> none  [the longest x1 136 us: across(): lax.all_to_all(lines, ('col', 'row'), split_axis=0, concat_axis=0, tiled=...]
    pallas_call x2, Pallas kernels: 21.2 us -> 158 us  [exchange(): pl.pallas_call(functools.partial(exchange_kernel, plan, back), in_specs=[...]
    all_to_all x3 -> x4, waiting for transfers between devices: 235 us -> 317 us  [across(): lax.all_to_all(lines, ('col', 'row'), split_axis=0, concat_axis=0, tiled=...]
    ppermute x7 -> x0, waiting for transfers between devices: 81.2 us -> none  [the longest x1 75.5 us: fast_term(): moved2 = lax.ppermute(moved, 'col', pairs[1])]
    all_to_all x5 -> x0, waiting for transfers between devices: 79.9 us -> none  [swap(): return lax.all_to_all(lines, 'row', split_axis=0, concat_axis=0, tiled=True)]
    all_to_all x3 -> x4, starting transfers between devices: 25.1 us -> 52.6 us  [across(): lax.all_to_all(lines, ('col', 'row'), split_axis=0, concat_axis=0, tiled=...]
    all_to_all x5 -> x0, starting transfers between devices: 24.8 us -> none  [swap(): return lax.all_to_all(lines, 'row', split_axis=0, concat_axis=0, tiled=True)]
    ppermute x7 -> x0, starting transfers between devices: 16.2 us -> none  [the longest x2 5.53 us: edge_of(): return lax.ppermute(side, 'row', [(1, 0), (2, 3)])]
  transfers between devices with their start and end apart: 15 -> 4, of which waited for: 9 -> 4; matrix products, arithmetic and copies ran while one was open for 7% -> 8% of each run, Pallas kernels for 14% -> 17%
where the time goes in v2:
time: 755 us; the launch traced here: 754 us
  waiting for transfers between devices  317 us (42%)
  Pallas kernels  312 us (41%)
  other arithmetic  72.2 us (10%)
  starting transfers between devices  52.6 us (7%)
    all_to_all x4, waiting for transfers between devices, across(): lax.all_to_all(lines, ('col', 'row'), split_axis=0, concat_axis=0, tiled=...  317 us
    pallas_call x2, Pallas kernels, exchange(): pl.pallas_call(functools.partial(exchange_kernel, plan, back), in_specs=[...  158 us
    pallas_call x2, Pallas kernels, columns(): pl.pallas_call(functools.partial(columns_kernel, plan), in_specs=[pl.Bloc...  114 us
    all_to_all x4, starting transfers between devices, across(): lax.all_to_all(lines, ('col', 'row'), split_axis=0, concat_axis=0, tiled=...  52.6 us
    pallas_call x2, Pallas kernels, lines_in(): pl.pallas_call(functools.partial(lines_in_kernel, plan, parity), grid=(sl...  24.2 us
    sub x1, other arithmetic, section_weights(): weight_c = 4.0 * phi_three - phi_two  22.8 us
    add x1, other arithmetic, fast_device(): damping * start_field + weight_a * start_term  21 us
    pallas_call x1, Pallas kernels, lines_out(): pl.pallas_call(functools.partial(lines_out_kernel, plan), grid=(slots,),...  15.3 us
  transfers between devices with their start and end apart: 4, of which 4 were waited for; matrix products, arithmetic and copies ran while one was open for 8% of the time, Pallas kernels for 17%

profile of v2, /device:TPU:9, one launch (start us, length us, event | category | flops | bytes accessed | tf_op | source)
XLA Modules:
  0.0 754.0 jit_solution(495744250920260543)
XLA Ops:
  0.8 1.0 multiply_cosine_fusion
  2.5 66.9 %home_lines.1.lines = f32[2,11,8,5632]{3,2,1,0:T(8,128)} custom-call(f32[2,16,4,8,2048]{4,3,2,1,0:T(8,128)} %bitcast.13), custom_call_target="tpu_custom_call" | custom-call | flops 17179869184 | bytes 16777216 | tf_op jit(solution)/shard_map/home_lines/pallas_call | solution.py:719
  69.5 1.3 add_bitcast_fusion.info
  70.8 0.8 fusion.94
  71.6 12.3 %lines_in.3 = f32[32,2,2,88,128]{4,3,2,1,0:T(8,128)} custom-call(s32[11]{0:T(128)} %add_bitcast_fusion.info, f32[2,11,8,5632]{3,2,1,0:T(8,128)} %home_lines.1.lines, f32[32,2,128]{2,1,0:T(2,128)} %get-tuple-element.23.turn, bf16[256,256]{1,0:T(8,128)(2,1)} %get-tuple-element.21.wh, bf16[256,256]{1,0:T(8,128)(2,1)} %get-tuple-element.22.wl), custom_call_target="tpu_custom_call" | custom-call | flops 4294967296 | bytes 16777216 | tf_op jit(solution)/shard_map/lines_in/pallas_call | solution.py:414
  83.9 24.6 %all-to-all-start.2 = ((f32[32,2,2,88,128]{4,3,2,1,0:T(8,128)}), f32[32,2,2,88,128]{4,3,2,1,0:T(8,128)}, u32[]{:S(2)}, u32[]{:S(2)}) async-start(f32[32,2,2,88,128]{4,3,2,1,0:T(8,128)} %lines_in.3), calls=%async_computation.2 | async-start | bytes 11534336 | tf_op jit(solution)/shard_map/all_to_all | solution.py:787
  108.5 11.9 %lines_in.2 = f32[32,2,2,88,128]{4,3,2,1,0:T(8,128)} custom-call(s32[11]{0:T(128)} %add_bitcast_fusion.info, f32[2,11,8,5632]{3,2,1,0:T(8,128)} %home_lines.1.lines, f32[32,2,128]{2,1,0:T(2,128)} %get-tuple-element.24.turn, bf16[256,256]{1,0:T(8,128)(2,1)} %get-tuple-element.21.wh, bf16[256,256]{1,0:T(8,128)(2,1)} %get-tuple-element.22.wl), custom_call_target="tpu_custom_call" | custom-call | flops 4294967296 | bytes 16777216 | tf_op jit(solution)/shard_map/lines_in/pallas_call | solution.py:414
  120.4 112.9 %all-to-all-done.2.src = f32[32,2,2,88,128]{4,3,2,1,0:T(8,128)} async-done(((f32[32,2,2,88,128]{4,3,2,1,0:T(8,128)}), f32[32,2,2,88,128]{4,3,2,1,0:T(8,128)}, u32[]{:S(2)}, u32[]{:S(2)}) %all-to-all-start.2) | async-done | bytes 5767200 | tf_op jit(solution)/shard_map/all_to_all | solution.py:787
  233.3 9.3 %all-to-all-start = ((f32[32,2,2,88,128]{4,3,2,1,0:T(8,128)}), f32[32,2,2,88,128]{4,3,2,1,0:T(8,128)}, u32[]{:S(2)}, u32[]{:S(2)}) async-start(f32[32,2,2,88,128]{4,3,2,1,0:T(8,128)} %lines_in.2), calls=%async_computation | async-start | bytes 11534336 | tf_op jit(solution)/shard_map/all_to_all | solution.py:787
  242.8 3.4 multiply_subtract_fusion
  246.3 4.5 fusion.1
  250.7 4.2 fusion
  254.9 57.1 %columns.3 = f32[32,2,2,88,128]{4,3,2,1,0:T(8,128)} custom-call(f32[32,2,2,88,128]{4,3,2,1,0:T(8,128)} %all-to-all-done.2.src, bf16[64,128,256]{2,1,0:T(8,128)(2,1)} %get-tuple-element.12.th, bf16[64,128,256]{2,1,0:T(8,128)(2,1)} %get-tuple-element.11.tl, bf16[64,256,128]{2,1,0:T(8,128)(2,1)} %get-tuple-element.10.fh, bf16[64,256,128]{2,1,0:T(8,128)(2,1)} %get-tuple-element.9.fl), custom_call_target="tpu_custom_call" | custom-call | flops 17179869184 | bytes 31457280 | tf_op jit(solution)/shard_map/columns/pallas_call | solution.py:498
  312.1 55.4 %all-to-all-done.src = f32[32,2,2,88,128]{4,3,2,1,0:T(8,128)} async-done(((f32[32,2,2,88,128]{4,3,2,1,0:T(8,128)}), f32[32,2,2,88,128]{4,3,2,1,0:T(8,128)}, u32[]{:S(2)}, u32[]{:S(2)}) %all-to-all-start) | async-done | bytes 5767200 | tf_op jit(solution)/shard_map/all_to_all | solution.py:787
  367.5 9.3 %all-to-all-start.3 = ((f32[32,2,2,88,128]{4,3,2,1,0:T(8,128)}), f32[32,2,2,88,128]{4,3,2,1,0:T(8,128)}, u32[]{:S(2)}, u32[]{:S(2)}) async-start(f32[32,2,2,88,128]{4,3,2,1,0:T(8,128)} %columns.3), calls=%async_computation.3 | async-start | bytes 11534336 | tf_op jit(solution)/shard_map/all_to_all | solution.py:787
  376.9 57.1 %columns.2 = f32[32,2,2,88,128]{4,3,2,1,0:T(8,128)} custom-call(f32[32,2,2,88,128]{4,3,2,1,0:T(8,128)} %all-to-all-done.src, bf16[64,128,256]{2,1,0:T(8,128)(2,1)} %get-tuple-element.12.th, bf16[64,128,256]{2,1,0:T(8,128)(2,1)} %get-tuple-element.11.tl, bf16[64,256,128]{2,1,0:T(8,128)(2,1)} %get-tuple-element.10.fh, bf16[64,256,128]{2,1,0:T(8,128)(2,1)} %get-tuple-element.9.fl), custom_call_target="tpu_custom_call" | custom-call | flops 17179869184 | bytes 31457280 | tf_op jit(solution)/shard_map/columns/pallas_call | solution.py:498
  434.0 67.7 %all-to-all-done.3.got1 = f32[32,2,2,88,128]{4,3,2,1,0:T(8,128)} async-done(((f32[32,2,2,88,128]{4,3,2,1,0:T(8,128)}), f32[32,2,2,88,128]{4,3,2,1,0:T(8,128)}, u32[]{:S(2)}, u32[]{:S(2)}) %all-to-all-start.3) | async-done | bytes 5767200 | tf_op jit(solution)/shard_map/all_to_all | solution.py:787
  501.7 9.4 %all-to-all-start.1 = ((f32[32,2,2,88,128]{4,3,2,1,0:T(8,128)}), f32[32,2,2,88,128]{4,3,2,1,0:T(8,128)}, u32[]{:S(2)}, u32[]{:S(2)}) async-start(f32[32,2,2,88,128]{4,3,2,1,0:T(8,128)} %columns.2), calls=%async_computation.1 | async-start | bytes 11534336 | tf_op jit(solution)/shard_map/all_to_all | solution.py:787
  511.1 22.8 %multiply_subtract_fusion.2 = (f32[512,2048]{1,0:T(8,128)}, f32[512,2048]{1,0:T(8,128)}, f32[512,2048]{1,0:T(8,128)}, f32[512,2048]{1,0:T(8,128)}) fusion(f32[512]{0:T(512)S(1)} %multiply_multiply_fusion.2, s32[2048]{0:T(1024)S(1)} %get-tuple-element.32, s32[2048]{0:T(1024)S(1)} %get-tuple-element.31, pred[2048]{0:T(1024)(128)(4,1)S(1)} %fusion.116, ...), kind=kLoop, calls=%fused_computation.110 | loop fusion | flops 102760448 | bytes 16799744 | tf_op jit(solution)/shard_map/sub | solution.py:46
  533.9 21.0 %multiply_add_fusion = f32[1,2,512,2048]{3,2,1,0:T(8,128)} fusion(f32[1,2,512,2048]{3,2,1,0:T(8,128)} %param.9, f32[1,2,512,2048]{3,2,1,0:T(8,128)} %param.10, f32[1,2,512,2048]{3,2,1,0:T(8,128)} %param.8, f32[1,2,512,2048]{3,2,1,0:T(8,128)} %param.6, f32[512,2048]{1,0:T(8,128)} %get-tuple-element.29, f32[512,2048]{1,0:T(8,128)} %get-tuple-element.28, ...), kind=kLoop, calls=%fused_computation.9 | loop fusion | flops 12582912 | bytes 54525952 | tf_op jit(solution)/shard_map/add | solution.py:811
  555.5 80.5 %all-to-all-done.1.got0 = f32[32,2,2,88,128]{4,3,2,1,0:T(8,128)} async-done(((f32[32,2,2,88,128]{4,3,2,1,0:T(8,128)}), f32[32,2,2,88,128]{4,3,2,1,0:T(8,128)}, u32[]{:S(2)}, u32[]{:S(2)}) %all-to-all-start.1) | async-done | bytes 5767200 | tf_op jit(solution)/shard_map/all_to_all | solution.py:787
  635.9 15.3 %lines_out.1.source = f32[2,11,8,5632]{3,2,1,0:T(8,128)} custom-call(s32[11]{0:T(128)} %add_bitcast_fusion.info, f32[32,2,2,88,128]{4,3,2,1,0:T(8,128)} %all-to-all-done.1.got0, f32[32,2,2,88,128]{4,3,2,1,0:T(8,128)} %all-to-all-done.3.got1, f32[2,32,2,128]{3,2,1,0:T(2,128)} %copy-done, bf16[256,256]{1,0:T(8,128)(2,1)} %get-tuple-element.14.wh, ...), custom_call_target="tpu_custom_call" | custom-call | flops 8589934592 | bytes 23068672 | tf_op jit(solution)/shard_map/lines_out/pallas_call | solution.py:556
  651.2 91.2 %lines_home.1 = f32[2,16,4,8,2048]{4,3,2,1,0:T(8,128)} custom-call(f32[2,11,8,5632]{3,2,1,0:T(8,128)} %lines_out.1.source), custom_call_target="tpu_custom_call" | custom-call | flops 17179869184 | bytes 16777216 | tf_op jit(solution)/shard_map/lines_home/pallas_call | solution.py:719
  742.4 11.6 %select_add_fusion = f32[1,2,512,2048]{3,2,1,0:T(8,128)} fusion(f32[1,2,512,2048]{3,2,1,0:T(8,128)} %multiply_add_fusion, f32[1,2,512,2048]{3,2,1,0:T(8,128)} %bitcast.11, f32[512,2048]{1,0:T(8,128)} %get-tuple-element.8, pred[512,2048]{1,0:T(8,128)(4,1)S(1)} %fusion.90), kind=kLoop, calls=%fused_computation.8 | loop fusion | flops 6291456 | bytes 30408704 | tf_op jit(solution)/shard_map/add | solution.py:818
  (15 shorter events, 2.2 us)
Async XLA Ops:
  1.9 67.6 %copy-start = (f32[2,32,2,128]{3,2,1,0:T(2,128)}, f32[2,32,2,128]{3,2,1,0:T(2,128)S(1)}, u32[]{:S(2)}) copy-start(f32[2,32,2,128]{3,2,1,0:T(2,128)S(1)} %maximum_bitcast_fusion.turn) | copy-start | bytes 196612
  83.9 149.4 %all-to-all-start.2 = ((f32[32,2,2,88,128]{4,3,2,1,0:T(8,128)}), f32[32,2,2,88,128]{4,3,2,1,0:T(8,128)}, u32[]{:S(2)}, u32[]{:S(2)}) async-start(f32[32,2,2,88,128]{4,3,2,1,0:T(8,128)} %lines_in.3), calls=%async_computation.2 | async-start | bytes 11534336 | tf_op jit(solution)/shard_map/all_to_all | solution.py:787
  233.3 134.2 %all-to-all-start = ((f32[32,2,2,88,128]{4,3,2,1,0:T(8,128)}), f32[32,2,2,88,128]{4,3,2,1,0:T(8,128)}, u32[]{:S(2)}, u32[]{:S(2)}) async-start(f32[32,2,2,88,128]{4,3,2,1,0:T(8,128)} %lines_in.2), calls=%async_computation | async-start | bytes 11534336 | tf_op jit(solution)/shard_map/all_to_all | solution.py:787
  367.5 134.2 %all-to-all-start.3 = ((f32[32,2,2,88,128]{4,3,2,1,0:T(8,128)}), f32[32,2,2,88,128]{4,3,2,1,0:T(8,128)}, u32[]{:S(2)}, u32[]{:S(2)}) async-start(f32[32,2,2,88,128]{4,3,2,1,0:T(8,128)} %columns.3), calls=%async_computation.3 | async-start | bytes 11534336 | tf_op jit(solution)/shard_map/all_to_all | solution.py:787
  501.7 134.2 %all-to-all-start.1 = ((f32[32,2,2,88,128]{4,3,2,1,0:T(8,128)}), f32[32,2,2,88,128]{4,3,2,1,0:T(8,128)}, u32[]{:S(2)}, u32[]{:S(2)}) async-start(f32[32,2,2,88,128]{4,3,2,1,0:T(8,128)} %columns.2), calls=%async_computation.1 | async-start | bytes 11534336 | tf_op jit(solution)/shard_map/all_to_all | solution.py:787

commit v3 on v2

--- a/solution.py
+++ b/solution.py
@@ -252,18 +252,16 @@
     raise ValueError("no place")
 
 
-def line_info(plan):
-    rows = []
+def first_line(plan, slot):
     slots, extra = plan["slots"], plan["extra"]
-    for col in range(plan["cols"]):
-        base = [col * plan["block_x"] + slot * plan["stride"] for slot in range(slots)]
-        for donor, taker, turn in plan["moves"]:
-            if taker == col:
-                start = slots - extra if turn == 0 else 0
-                for step in range(extra):
-                    base[start + step] = donor * plan["block_x"] + (slots + step) * plan["stride"]
-        rows.append(base)
-    return rows
+    col = lax.axis_index("col")
+    base = col * plan["block_x"] + slot * plan["stride"]
+    for donor, taker, turn in plan["moves"]:
+        start = slots - extra if turn == 0 else 0
+        moved = donor * plan["block_x"] + (slots + slot - start) * plan["stride"]
+        here = (col == taker) & (slot >= start) & (slot < start + extra)
+        base = jnp.where(here, moved, base)
+    return base + lax.axis_index("row") * SUBL
 
 
 def cadd(a, b):
@@ -361,52 +359,78 @@
     return (3 * wave_x < plan["length"]) & (3 * jnp.abs(wave_y) < plan["length"])
 
 
-def lines_in_kernel(plan, parity, info, lines, turn, wh, wl, out, scr):
+def fetch_slots(slots, pairs, sems):
+    j = pl.program_id(0)
+
+    def copy(n, slot):
+        source, held = pairs[n]
+        return pltpu.make_async_copy(source.at[:, slot], held.at[slot], sems.at[n, slot])
+
+    @pl.when(j == 0)
+    def _():
+        @pl.loop(0, slots)
+        def _(slot):
+            for n in range(len(pairs)):
+                copy(n, slot).start()
+
+    for n in range(len(pairs)):
+        copy(n, j).wait()
+    return j
+
+
+def lines_in_kernel(plan, parity, lines, turn, wh, wl, out, psi, scr, held, sems):
     length = plan["length"]
-    j = pl.program_id(0)
-    wave_x = info[j] + sublane_iota()
+    j = fetch_slots(plan["slots"], [(lines, held)], sems)
+    half = HALF // 2
+    wave_x = first_line(plan, pl.program_id(0)) + sublane_iota()
     kx = wave_x.astype(jnp.float32)
+    kx_sq = kx * kx
     doubled = jnp.where(wave_x == 0, 1.0, 2.0) * (length / 9.0)
     step = wave_scale / length
-    lane = lane_iota()
+    lane = lane_iota().astype(jnp.float32)
+    keep_x = 3 * wave_x < length
+    tiles = kept_tiles(plan)
+    edges = (plan["low"] - 1, HALF - plan["low"])
+
+    def ky_of(a):
+        return lane + float(LANES * a - (length if a >= half else 0))
+
+    for t, a in enumerate(tiles):
+        off = tile_of(plan, a)
+        ky = ky_of(a)
+        factor = doubled / jnp.maximum(kx_sq + ky * ky, 1.0)
+        keep = keep_x & (3.0 * jnp.abs(ky) < length) if a in edges else keep_x
+        re, im = (jnp.where(keep, held[j, p, :, off:off + LANES], 0.0) for p in range(2))
+        psi[t, 0] = -factor * im
+        psi[t, 1] = factor * re
     for field in range(2):
-        tiles = {}
-        for a in kept_tiles(plan):
-            off = tile_of(plan, a)
-            wave_y = lane + (LANES * a - (length if a >= HALF // 2 else 0))
-            square = (wave_x * wave_x + wave_y * wave_y)
-            factor = doubled / jnp.maximum(square, 1).astype(jnp.float32)
-            keep = keep_of(plan, wave_x, wave_y)
-            if field == 0:
-                factor = factor * (step * wave_y.astype(jnp.float32))
-            else:
-                factor = factor * (-step * kx)
-            parts = []
-            for p in range(2):
-                parts.append(jnp.where(keep, lines[p, 0, :, off:off + LANES], 0.0))
-            tiles[a] = (-factor * parts[1], factor * parts[0])
+        values = {}
+        for t, a in enumerate(tiles):
+            weight = step * ky_of(a) if field == 0 else -step * kx
+            values[a] = (psi[t, 0] * weight, psi[t, 1] * weight)
         mixed = []
-        for a in range(HALF // 2):
-            x0, x1 = tiles.get(a), tiles.get(a + HALF // 2)
+        for a in range(half):
+            x0, x1 = values.get(a), values.get(a + half)
             if parity == 0:
                 mixed.append(cadd(x0, x1))
             else:
                 mixed.append(cturn(csub(x0, x1), a, HALF, 1))
-        result = butterflies(mixed, 1, range(HALF // 2))
-        for e in range(HALF // 2):
+        result = butterflies(mixed, 1, range(half))
+        for e in range(half):
             re, im = result[e]
             cosine, sine_part = turn[e, 0:1, :], turn[e, 1:2, :]
-            at = slice(SUBL * e, SUBL * (e + 1))
+            first = (field * half + e) * SUBL
+            at = slice(first, first + SUBL)
             scr[at, 0:LANES] = re * cosine - im * sine_part
             scr[at, LANES:] = re * sine_part + im * cosine
-        spread = dot3(halves(scr[...]), (wh[...], wl[...]))
+    spread = dot3(halves(scr[...]), (wh[...], wl[...]))
+    for field in range(2):
+        rows = spread[field * half * SUBL:(field + 1) * half * SUBL]
         for s in range(2):
-            out[:, field, s] = spread[:, s * LANES:(s + 1) * LANES].reshape(
-                HALF // 2, SUBL, LANES
-            )
-
-
-def lines_in(plan, parity, info, lines, turn, table):
+            out[:, 0, field, s] = rows[:, s * LANES:(s + 1) * LANES].reshape(half, SUBL, LANES)
+
+
+def lines_in(plan, parity, lines, turn, table):
     slots = plan["slots"]
     width = 2 * plan["low"] * LANES
     devices = plan["rows"] * plan["cols"]
@@ -415,19 +439,23 @@
         functools.partial(lines_in_kernel, plan, parity),
         grid=(slots,),
         in_specs=[
-            pl.BlockSpec(memory_space=pltpu.SMEM),
-            pl.BlockSpec((2, 1, SUBL, width), lambda j: (0, j, 0, 0)),
+            pl.BlockSpec(memory_space=pl.ANY),
             whole((HALF // 2, 2, LANES)),
             whole((2 * LANES, 2 * LANES)),
             whole((2 * LANES, 2 * LANES)),
         ],
-        out_specs=pl.BlockSpec((devices, 2, 2, SUBL, LANES), lambda j: (0, 0, 0, j, 0)),
-        out_shape=jax.ShapeDtypeStruct((devices, 2, 2, slots * SUBL, LANES), jnp.float32),
-        scratch_shapes=[pltpu.VMEM((HALF // 2 * SUBL, 2 * LANES), jnp.float32)],
+        out_specs=pl.BlockSpec((devices, 1, 2, 2, SUBL, LANES), lambda j: (0, j, 0, 0, 0, 0)),
+        out_shape=jax.ShapeDtypeStruct((devices, slots, 2, 2, SUBL, LANES), jnp.float32),
+        scratch_shapes=[
+            pltpu.VMEM((2 * plan["low"], 2, SUBL, LANES), jnp.float32),
+            pltpu.VMEM((HALF * SUBL, 2 * LANES), jnp.float32),
+            pltpu.VMEM((slots, 2, SUBL, width), jnp.float32),
+            pltpu.SemaphoreType.DMA((1, slots)),
+        ],
         compiler_params=pltpu.CompilerParams(vmem_limit_bytes=60 << 20),
         cost_estimate=pl.CostEstimate(flops=4 << 30, bytes_accessed=16 << 20, transcendentals=0),
         name="lines_in",
-    )(info, lines, turn, *table)
+    )(lines, turn, *table)
 
 
 def columns_kernel(plan, src, th, tl, fh, fl, out, mid):
@@ -450,9 +478,8 @@
                 if place is None:
                     values.append(None)
                     continue
-                at = pl.ds(place[1] * SUBL, SUBL)
-                dev = place[0] * rows + r
-                values.append((src[dev, field, 0, at, :], src[dev, field, 1, at, :]))
+                at = (place[0] * rows + r, place[1], field)
+                values.append((src[at + (0,)], src[at + (1,)]))
             result = butterflies(values, 1, range(HALF))
             base = pl.multiple_of((q * rows + r) * SUBL, SUBL)
             for c in range(HALF):
@@ -481,15 +508,14 @@
             result = butterflies(values, -1, need)
             for a in need:
                 place = inside[q][a]
-                at = pl.ds(place[1] * SUBL, SUBL)
-                dev = place[0] * rows + r
-                out[dev, field, 0, at, :] = result[a][0]
-                out[dev, field, 1, at, :] = result[a][1]
+                at = (place[0] * rows + r, place[1], field)
+                out[at + (0,)] = result[a][0]
+                out[at + (1,)] = result[a][1]
         for col in range(plan["cols"]):
             for slot in range(plan["slots"]):
                 if (col, slot) not in used:
                     for p in range(2):
-                        out[col * rows + r, field, p, pl.ds(slot * SUBL, SUBL), :] = jnp.zeros(
+                        out[col * rows + r, slot, field, p] = jnp.zeros(
                             (SUBL, LANES), jnp.float32
                         )
 
@@ -507,57 +533,64 @@
     )(spread, *tables)
 
 
-def lines_out_kernel(plan, info, got0, got1, turn, wh, wl, lines, scr, acc):
+def lines_out_kernel(plan, got0, got1, turn, wh, wl, lines, scr, acc, held0, held1, sems):
     length = plan["length"]
-    j = pl.program_id(0)
-    wave_x = info[j] + sublane_iota()
+    j = fetch_slots(plan["slots"], [(got0, held0), (got1, held1)], sems)
+    half = HALF // 2
+    wave_x = first_line(plan, pl.program_id(0)) + sublane_iota()
     step = wave_scale / length
     kappa_x = step * wave_x.astype(jnp.float32)
-    lane = lane_iota()
+    kappa_x_sq = kappa_x * kappa_x
+    lane = lane_iota().astype(jnp.float32)
+    keep_x = 3 * wave_x < length
     tiles = kept_tiles(plan)
-    rows = HALF // 2 * SUBL
+    edges = (plan["low"] - 1, HALF - plan["low"])
+    rows = half * SUBL
+    both = jnp.concatenate(
+        [
+            jnp.concatenate([held[j, :, field, s].reshape(rows, LANES) for s in range(2)], axis=1)
+            for field in range(2) for held in (held0, held1)
+        ],
+        axis=0,
+    )
+    scr[...] = dot3(halves(both), (wh[...], wl[...]))
     for field in range(2):
-        for parity, got in enumerate((got0, got1)):
-            both = jnp.concatenate(
-                [got[:, field, s].reshape(rows, LANES) for s in range(2)], axis=1
-            )
-            scr[parity] = dot3(halves(both), (wh[...], wl[...]))
         values = []
         for c in range(HALF):
             e, parity = c // 2, c % 2
-            at = slice(SUBL * e, SUBL * (e + 1))
-            re, im = scr[parity, at, 0:LANES], scr[parity, at, LANES:]
+            first = ((2 * field + parity) * half + e) * SUBL
+            at = slice(first, first + SUBL)
+            re, im = scr[at, 0:LANES], scr[at, LANES:]
             cosine, sine_part = turn[parity, e, 0:1, :], turn[parity, e, 1:2, :]
             values.append((re * cosine + im * sine_part, im * cosine - re * sine_part))
         result = butterflies(values, -1, tiles)
         for t, a in enumerate(tiles):
-            wave_y = lane + (LANES * a - (length if a >= HALF // 2 else 0))
-            kappa_y = step * wave_y.astype(jnp.float32)
-            keep = keep_of(plan, wave_x, wave_y)
+            ky = lane + float(LANES * a - (length if a >= half else 0))
+            kappa_y = step * ky
             if field == 0:
-                weight = (kappa_x * kappa_x - kappa_y * kappa_y) * (1.0 / length)
+                weight = (kappa_x_sq - kappa_y * kappa_y) * (1.0 / length)
             else:
                 weight = kappa_x * kappa_y * (1.0 / length)
+            keep = keep_x & (3.0 * jnp.abs(ky) < length) if a in edges else keep_x
             off = tile_of(plan, a)
             for p in range(2):
-                value = jnp.where(keep, weight * result[a][p], 0.0)
+                value = weight * result[a][p]
                 if field == 0:
                     acc[t, p] = value
                 else:
-                    lines[p, 0, :, off:off + LANES] = acc[t, p] + value
-
-
-def lines_out(plan, info, got0, got1, turn, table):
+                    lines[p, 0, :, off:off + LANES] = jnp.where(keep, acc[t, p] + value, 0.0)
+
+
+def lines_out(plan, got0, got1, turn, table):
     slots = plan["slots"]
     width = 2 * plan["low"] * LANES
     devices = plan["rows"] * plan["cols"]
     whole = lambda shape: pl.BlockSpec(shape, lambda j: (0,) * len(shape))
-    got_spec = pl.BlockSpec((devices, 2, 2, SUBL, LANES), lambda j: (0, 0, 0, j, 0))
+    got_spec = pl.BlockSpec(memory_space=pl.ANY)
     return pl.pallas_call(
         functools.partial(lines_out_kernel, plan),
         grid=(slots,),
         in_specs=[
-            pl.BlockSpec(memory_space=pltpu.SMEM),
             got_spec,
             got_spec,
             whole((2, HALF // 2, 2, LANES)),
@@ -567,13 +600,16 @@
         out_specs=pl.BlockSpec((2, 1, SUBL, width), lambda j: (0, j, 0, 0)),
         out_shape=jax.ShapeDtypeStruct((2, slots, SUBL, width), jnp.float32),
         scratch_shapes=[
-            pltpu.VMEM((2, HALF // 2 * SUBL, 2 * LANES), jnp.float32),
+            pltpu.VMEM((2 * HALF * SUBL, 2 * LANES), jnp.float32),
             pltpu.VMEM((2 * plan["low"], 2, SUBL, LANES), jnp.float32),
+            pltpu.VMEM((slots, devices, 2, 2, SUBL, LANES), jnp.float32),
+            pltpu.VMEM((slots, devices, 2, 2, SUBL, LANES), jnp.float32),
+            pltpu.SemaphoreType.DMA((2, slots)),
         ],
         compiler_params=pltpu.CompilerParams(vmem_limit_bytes=60 << 20),
         cost_estimate=pl.CostEstimate(flops=8 << 30, bytes_accessed=22 << 20, transcendentals=0),
         name="lines_out",
-    )(info, got0, got1, turn, *table)
+    )(got0, got1, turn, *table)
 
 
 def spans(plan, row):
@@ -780,8 +816,6 @@
 
 def fast_term(plan, field):
     rows = plan["rows"]
-    row, col = lax.axis_index("row"), lax.axis_index("col")
-    info = jnp.asarray(line_info(plan), jnp.int32)[col] + (row * SUBL).astype(jnp.int32)
 
     def across(lines):
         return lax.all_to_all(lines, ("col", "row"), split_axis=0, concat_axis=0, tiled=True)
@@ -791,11 +825,11 @@
     turn = turns(plan["length"])
     table = lane_table(1.0)
     spread = [
-        across(lines_in(plan, parity, info, lines, turn[parity], table)) for parity in range(2)
+        across(lines_in(plan, parity, lines, turn[parity], table)) for parity in range(2)
     ]
     tables = column_tables(plan["length"])
     back = [across(columns(plan, part, tables)) for part in spread]
-    lines = lines_out(plan, info, *back, turn, lane_table(-1.0))
+    lines = lines_out(plan, *back, turn, lane_table(-1.0))
     return exchange(plan, True, lines).reshape(field.shape)
 
 

time: 755 us -> 751 us (level)
  no operation moved by 1% of the time
where the time goes in v3:
time: 751 us; the launch traced here: 750 us
  waiting for transfers between devices  318 us (42%)
  Pallas kernels  308 us (41%)
  other arithmetic  70.9 us (9%)
  starting transfers between devices  52.6 us (7%)
    all_to_all x4, waiting for transfers between devices, across(): lax.all_to_all(lines, ('col', 'row'), split_axis=0, concat_axis=0, tiled=...  318 us
    pallas_call x2, Pallas kernels, exchange(): pl.pallas_call(functools.partial(exchange_kernel, plan, back), in_specs=[...  158 us
    pallas_call x2, Pallas kernels, columns(): pl.pallas_call(functools.partial(columns_kernel, plan), in_specs=[pl.Bloc...  114 us
    all_to_all x4, starting transfers between devices, across(): lax.all_to_all(lines, ('col', 'row'), split_axis=0, concat_axis=0, tiled=...  52.6 us
    sub x1, other arithmetic, section_weights(): weight_c = 4.0 * phi_three - phi_two  22.8 us
    pallas_call x2, Pallas kernels, lines_in(): pl.pallas_call(functools.partial(lines_in_kernel, plan, parity), grid=(sl...  21.3 us
    add x1, other arithmetic, fast_device(): damping * start_field + weight_a * start_term  21 us
  transfers between devices with their start and end apart: 4, of which 4 were waited for; matrix products, arithmetic and copies ran while one was open for 8% of the time, Pallas kernels for 17%

profile of v3, /device:TPU:9, one launch (start us, length us, event | category | flops | bytes accessed | tf_op | source)
XLA Modules:
  0.0 750.3 jit_solution(3668980293352765375)
XLA Ops:
  0.8 1.0 multiply_cosine_fusion
  1.9 0.6 slice_bitcast_fusion
  2.5 66.9 %home_lines.1.lines = f32[2,11,8,5632]{3,2,1,0:T(8,128)} custom-call(f32[2,16,4,8,2048]{4,3,2,1,0:T(8,128)} %bitcast.11), custom_call_target="tpu_custom_call" | custom-call | flops 17179869184 | bytes 16777216 | tf_op jit(solution)/shard_map/home_lines/pallas_call | solution.py:755
  69.5 0.8 fusion.94
  70.3 10.9 %lines_in.3 = f32[32,11,2,2,8,128]{5,4,3,2,1,0:T(8,128)} custom-call(f32[2,11,8,5632]{3,2,1,0:T(8,128)} %home_lines.1.lines, f32[32,2,128]{2,1,0:T(2,128)} %get-tuple-element.23.turn, bf16[256,256]{1,0:T(8,128)(2,1)} %get-tuple-element.21.wh, bf16[256,256]{1,0:T(8,128)(2,1)} %get-tuple-element.22.wl), custom_call_target="tpu_custom_call" | custom-call | flops 4294967296 | bytes 16777216 | tf_op jit(solution)/shard_map/lines_in/pallas_call | solution.py:438
  81.3 24.6 %all-to-all-start.2 = ((f32[32,11,2,2,8,128]{5,4,3,2,1,0:T(8,128)}), f32[32,11,2,2,8,128]{5,4,3,2,1,0:T(8,128)}, u32[]{:S(2)}, u32[]{:S(2)}) async-start(f32[32,11,2,2,8,128]{5,4,3,2,1,0:T(8,128)} %lines_in.3), calls=%async_computation.2 | async-start | bytes 11534336 | tf_op jit(solution)/shard_map/all_to_all | solution.py:821
  105.8 10.4 %lines_in.2 = f32[32,11,2,2,8,128]{5,4,3,2,1,0:T(8,128)} custom-call(f32[2,11,8,5632]{3,2,1,0:T(8,128)} %home_lines.1.lines, f32[32,2,128]{2,1,0:T(2,128)} %get-tuple-element.24.turn, bf16[256,256]{1,0:T(8,128)(2,1)} %get-tuple-element.21.wh, bf16[256,256]{1,0:T(8,128)(2,1)} %get-tuple-element.22.wl), custom_call_target="tpu_custom_call" | custom-call | flops 4294967296 | bytes 16777216 | tf_op jit(solution)/shard_map/lines_in/pallas_call | solution.py:438
  116.2 114.4 %all-to-all-done.2.src = f32[32,11,2,2,8,128]{5,4,3,2,1,0:T(8,128)} async-done(((f32[32,11,2,2,8,128]{5,4,3,2,1,0:T(8,128)}), f32[32,11,2,2,8,128]{5,4,3,2,1,0:T(8,128)}, u32[]{:S(2)}, u32[]{:S(2)}) %all-to-all-start.2) | async-done | bytes 5767200 | tf_op jit(solution)/shard_map/all_to_all | solution.py:821
  230.7 9.3 %all-to-all-start = ((f32[32,11,2,2,8,128]{5,4,3,2,1,0:T(8,128)}), f32[32,11,2,2,8,128]{5,4,3,2,1,0:T(8,128)}, u32[]{:S(2)}, u32[]{:S(2)}) async-start(f32[32,11,2,2,8,128]{5,4,3,2,1,0:T(8,128)} %lines_in.2), calls=%async_computation | async-start | bytes 11534336 | tf_op jit(solution)/shard_map/all_to_all | solution.py:821
  240.2 3.4 multiply_subtract_fusion
  243.6 4.5 fusion.1
  248.1 4.2 fusion
  252.3 57.1 %columns.3 = f32[32,11,2,2,8,128]{5,4,3,2,1,0:T(8,128)} custom-call(f32[32,11,2,2,8,128]{5,4,3,2,1,0:T(8,128)} %all-to-all-done.2.src, bf16[64,128,256]{2,1,0:T(8,128)(2,1)} %get-tuple-element.12.th, bf16[64,128,256]{2,1,0:T(8,128)(2,1)} %get-tuple-element.11.tl, bf16[64,256,128]{2,1,0:T(8,128)(2,1)} %get-tuple-element.10.fh, ...), custom_call_target="tpu_custom_call" | custom-call | flops 17179869184 | bytes 31457280 | tf_op jit(solution)/shard_map/columns/pallas_call | solution.py:524
  309.4 55.4 %all-to-all-done.src = f32[32,11,2,2,8,128]{5,4,3,2,1,0:T(8,128)} async-done(((f32[32,11,2,2,8,128]{5,4,3,2,1,0:T(8,128)}), f32[32,11,2,2,8,128]{5,4,3,2,1,0:T(8,128)}, u32[]{:S(2)}, u32[]{:S(2)}) %all-to-all-start) | async-done | bytes 5767200 | tf_op jit(solution)/shard_map/all_to_all | solution.py:821
  364.9 9.3 %all-to-all-start.3 = ((f32[32,11,2,2,8,128]{5,4,3,2,1,0:T(8,128)}), f32[32,11,2,2,8,128]{5,4,3,2,1,0:T(8,128)}, u32[]{:S(2)}, u32[]{:S(2)}) async-start(f32[32,11,2,2,8,128]{5,4,3,2,1,0:T(8,128)} %columns.3), calls=%async_computation.3 | async-start | bytes 11534336 | tf_op jit(solution)/shard_map/all_to_all | solution.py:821
  374.2 57.2 %columns.2 = f32[32,11,2,2,8,128]{5,4,3,2,1,0:T(8,128)} custom-call(f32[32,11,2,2,8,128]{5,4,3,2,1,0:T(8,128)} %all-to-all-done.src, bf16[64,128,256]{2,1,0:T(8,128)(2,1)} %get-tuple-element.12.th, bf16[64,128,256]{2,1,0:T(8,128)(2,1)} %get-tuple-element.11.tl, bf16[64,256,128]{2,1,0:T(8,128)(2,1)} %get-tuple-element.10.fh, ...), custom_call_target="tpu_custom_call" | custom-call | flops 17179869184 | bytes 31457280 | tf_op jit(solution)/shard_map/columns/pallas_call | solution.py:524
  431.4 67.7 %all-to-all-done.3.got1 = f32[32,11,2,2,8,128]{5,4,3,2,1,0:T(8,128)} async-done(((f32[32,11,2,2,8,128]{5,4,3,2,1,0:T(8,128)}), f32[32,11,2,2,8,128]{5,4,3,2,1,0:T(8,128)}, u32[]{:S(2)}, u32[]{:S(2)}) %all-to-all-start.3) | async-done | bytes 5767200 | tf_op jit(solution)/shard_map/all_to_all | solution.py:821
  499.0 9.4 %all-to-all-start.1 = ((f32[32,11,2,2,8,128]{5,4,3,2,1,0:T(8,128)}), f32[32,11,2,2,8,128]{5,4,3,2,1,0:T(8,128)}, u32[]{:S(2)}, u32[]{:S(2)}) async-start(f32[32,11,2,2,8,128]{5,4,3,2,1,0:T(8,128)} %columns.2), calls=%async_computation.1 | async-start | bytes 11534336 | tf_op jit(solution)/shard_map/all_to_all | solution.py:821
  508.5 22.8 %multiply_subtract_fusion.2 = (f32[512,2048]{1,0:T(8,128)}, f32[512,2048]{1,0:T(8,128)}, f32[512,2048]{1,0:T(8,128)}, f32[512,2048]{1,0:T(8,128)}) fusion(f32[512]{0:T(512)S(1)} %multiply_multiply_fusion.2, s32[2048]{0:T(1024)S(1)} %get-tuple-element.32, s32[2048]{0:T(1024)S(1)} %get-tuple-element.31, pred[2048]{0:T(1024)(128)(4,1)S(1)} %fusion.116, ...), kind=kLoop, calls=%fused_computation.110 | loop fusion | flops 102760448 | bytes 16799744 | tf_op jit(solution)/shard_map/sub | solution.py:46
  531.3 21.0 %multiply_add_fusion = f32[1,2,512,2048]{3,2,1,0:T(8,128)} fusion(f32[1,2,512,2048]{3,2,1,0:T(8,128)} %param.8, f32[1,2,512,2048]{3,2,1,0:T(8,128)} %param.9, f32[1,2,512,2048]{3,2,1,0:T(8,128)} %param.7, f32[1,2,512,2048]{3,2,1,0:T(8,128)} %param.5, f32[512,2048]{1,0:T(8,128)} %get-tuple-element.29, f32[512,2048]{1,0:T(8,128)} %get-tuple-element.28, ...), kind=kLoop, calls=%fused_computation.9 | loop fusion | flops 12582912 | bytes 54525952 | tf_op jit(solution)/shard_map/add | solution.py:845
  552.8 80.5 %all-to-all-done.1.got0 = f32[32,11,2,2,8,128]{5,4,3,2,1,0:T(8,128)} async-done(((f32[32,11,2,2,8,128]{5,4,3,2,1,0:T(8,128)}), f32[32,11,2,2,8,128]{5,4,3,2,1,0:T(8,128)}, u32[]{:S(2)}, u32[]{:S(2)}) %all-to-all-start.1) | async-done | bytes 5767200 | tf_op jit(solution)/shard_map/all_to_all | solution.py:821
  633.3 14.2 %lines_out.1.source = f32[2,11,8,5632]{3,2,1,0:T(8,128)} custom-call(f32[32,11,2,2,8,128]{5,4,3,2,1,0:T(8,128)} %all-to-all-done.1.got0, f32[32,11,2,2,8,128]{5,4,3,2,1,0:T(8,128)} %all-to-all-done.3.got1, f32[2,32,2,128]{3,2,1,0:T(2,128)} %copy-done, bf16[256,256]{1,0:T(8,128)(2,1)} %get-tuple-element.14.wh, bf16[256,256]{1,0:T(8,128)(2,1)} %get-tuple-element.13.wl), custom_call_target="tpu_custom_call" | custom-call | flops 8589934592 | bytes 23068672 | tf_op jit(solution)/shard_map/lines_out/pallas_call | solution.py:590
  647.5 91.2 %lines_home.1 = f32[2,16,4,8,2048]{4,3,2,1,0:T(8,128)} custom-call(f32[2,11,8,5632]{3,2,1,0:T(8,128)} %lines_out.1.source), custom_call_target="tpu_custom_call" | custom-call | flops 17179869184 | bytes 16777216 | tf_op jit(solution)/shard_map/lines_home/pallas_call | solution.py:755
  738.7 11.6 %select_add_fusion = f32[1,2,512,2048]{3,2,1,0:T(8,128)} fusion(f32[1,2,512,2048]{3,2,1,0:T(8,128)} %multiply_add_fusion, f32[1,2,512,2048]{3,2,1,0:T(8,128)} %bitcast.9, f32[512,2048]{1,0:T(8,128)} %get-tuple-element.8, pred[512,2048]{1,0:T(8,128)(4,1)S(1)} %fusion.90), kind=kLoop, calls=%fused_computation.8 | loop fusion | flops 6291456 | bytes 30408704 | tf_op jit(solution)/shard_map/add | solution.py:852
  (14 shorter events, 1.6 us)
Async XLA Ops:
  1.9 67.6 %copy-start = (f32[2,32,2,128]{3,2,1,0:T(2,128)}, f32[2,32,2,128]{3,2,1,0:T(2,128)S(1)}, u32[]{:S(2)}) copy-start(f32[2,32,2,128]{3,2,1,0:T(2,128)S(1)} %maximum_bitcast_fusion.turn) | copy-start | bytes 196612
  81.3 149.4 %all-to-all-start.2 = ((f32[32,11,2,2,8,128]{5,4,3,2,1,0:T(8,128)}), f32[32,11,2,2,8,128]{5,4,3,2,1,0:T(8,128)}, u32[]{:S(2)}, u32[]{:S(2)}) async-start(f32[32,11,2,2,8,128]{5,4,3,2,1,0:T(8,128)} %lines_in.3), calls=%async_computation.2 | async-start | bytes 11534336 | tf_op jit(solution)/shard_map/all_to_all | solution.py:821
  230.7 134.2 %all-to-all-start = ((f32[32,11,2,2,8,128]{5,4,3,2,1,0:T(8,128)}), f32[32,11,2,2,8,128]{5,4,3,2,1,0:T(8,128)}, u32[]{:S(2)}, u32[]{:S(2)}) async-start(f32[32,11,2,2,8,128]{5,4,3,2,1,0:T(8,128)} %lines_in.2), calls=%async_computation | async-start | bytes 11534336 | tf_op jit(solution)/shard_map/all_to_all | solution.py:821
  364.9 134.2 %all-to-all-start.3 = ((f32[32,11,2,2,8,128]{5,4,3,2,1,0:T(8,128)}), f32[32,11,2,2,8,128]{5,4,3,2,1,0:T(8,128)}, u32[]{:S(2)}, u32[]{:S(2)}) async-start(f32[32,11,2,2,8,128]{5,4,3,2,1,0:T(8,128)} %columns.3), calls=%async_computation.3 | async-start | bytes 11534336 | tf_op jit(solution)/shard_map/all_to_all | solution.py:821
  499.0 134.2 %all-to-all-start.1 = ((f32[32,11,2,2,8,128]{5,4,3,2,1,0:T(8,128)}), f32[32,11,2,2,8,128]{5,4,3,2,1,0:T(8,128)}, u32[]{:S(2)}, u32[]{:S(2)}) async-start(f32[32,11,2,2,8,128]{5,4,3,2,1,0:T(8,128)} %columns.2), calls=%async_computation.1 | async-start | bytes 11534336 | tf_op jit(solution)/shard_map/all_to_all | solution.py:821

commit v4 on v3

--- a/solution.py
+++ b/solution.py
@@ -533,11 +533,10 @@
     )(spread, *tables)
 
 
-def lines_out_kernel(plan, got0, got1, turn, wh, wl, lines, scr, acc, held0, held1, sems):
+def slot_out(plan, j, held0, held1, turn, wh, wl, lines, scr, acc):
     length = plan["length"]
-    j = fetch_slots(plan["slots"], [(got0, held0), (got1, held1)], sems)
     half = HALF // 2
-    wave_x = first_line(plan, pl.program_id(0)) + sublane_iota()
+    wave_x = first_line(plan, j) + sublane_iota()
     step = wave_scale / length
     kappa_x = step * wave_x.astype(jnp.float32)
     kappa_x_sq = kappa_x * kappa_x
@@ -578,38 +577,7 @@
                 if field == 0:
                     acc[t, p] = value
                 else:
-                    lines[p, 0, :, off:off + LANES] = jnp.where(keep, acc[t, p] + value, 0.0)
-
-
-def lines_out(plan, got0, got1, turn, table):
-    slots = plan["slots"]
-    width = 2 * plan["low"] * LANES
-    devices = plan["rows"] * plan["cols"]
-    whole = lambda shape: pl.BlockSpec(shape, lambda j: (0,) * len(shape))
-    got_spec = pl.BlockSpec(memory_space=pl.ANY)
-    return pl.pallas_call(
-        functools.partial(lines_out_kernel, plan),
-        grid=(slots,),
-        in_specs=[
-            got_spec,
-            got_spec,
-            whole((2, HALF // 2, 2, LANES)),
-            whole((2 * LANES, 2 * LANES)),
-            whole((2 * LANES, 2 * LANES)),
-        ],
-        out_specs=pl.BlockSpec((2, 1, SUBL, width), lambda j: (0, j, 0, 0)),
-        out_shape=jax.ShapeDtypeStruct((2, slots, SUBL, width), jnp.float32),
-        scratch_shapes=[
-            pltpu.VMEM((2 * HALF * SUBL, 2 * LANES), jnp.float32),
-            pltpu.VMEM((2 * plan["low"], 2, SUBL, LANES), jnp.float32),
-            pltpu.VMEM((slots, devices, 2, 2, SUBL, LANES), jnp.float32),
-            pltpu.VMEM((slots, devices, 2, 2, SUBL, LANES), jnp.float32),
-            pltpu.SemaphoreType.DMA((2, slots)),
-        ],
-        compiler_params=pltpu.CompilerParams(vmem_limit_bytes=60 << 20),
-        cost_estimate=pl.CostEstimate(flops=8 << 30, bytes_accessed=22 << 20, transcendentals=0),
-        name="lines_out",
-    )(got0, got1, turn, *table)
+                    lines[j, p, :, off:off + LANES] = jnp.where(keep, acc[t, p] + value, 0.0)
 
 
 def spans(plan, row):
@@ -767,6 +735,160 @@
     )(source)
 
 
+def lines_home_kernel(
+    plan, got0, got1, turn, wh, wl, home, scr, acc, held0, held1, lines, sems, send, recv
+):
+    rows, slots, extra = plan["rows"], plan["slots"], plan["extra"]
+    row, col = lax.axis_index("row"), lax.axis_index("col")
+    pairs = ((got0, held0), (got1, held1))
+
+    def fetch(n, slot):
+        source, held = pairs[n]
+        return pltpu.make_async_copy(source.at[:, slot], held.at[slot], sems.at[n, slot])
+
+    def slot_of(i):
+        return lax.rem(i + slots - extra, slots)
+
+    def each(home_row, act):
+        act(0)
+
+        @pl.when(both_of(home_row))
+        def _():
+            act(1)
+
+    def remote(source, target, kind, step, piece, where):
+        return pltpu.make_async_remote_copy(
+            src_ref=source, dst_ref=target, send_sem=send.at[kind, step, piece],
+            recv_sem=recv.at[kind, step, piece], device_id=where,
+            device_id_type=pl.DeviceIdType.MESH,
+        )
+
+    def put(slot, group, kind, where):
+        for step in range(rows):
+            other = (row + step) % rows
+
+            def act(piece):
+                home_at, line_at, width = spans(plan, other)[piece]
+                source = lines.at[slot, :, :, pl.ds(line_at, width)]
+                target = home.at[:, group, row, :, pl.ds(home_at, width)]
+                if kind == 0 and step == 0:
+                    pltpu.make_async_copy(source, target, send.at[0, 0, piece]).start()
+                else:
+                    remote(source, target, kind, step, piece, where(other)).start()
+
+            each(other, act)
+
+    def put_slot(slot):
+        for donor, taker, turn_id in plan["moves"]:
+            start = slots - extra if turn_id == 0 else 0
+
+            @pl.when((col == taker) & (slot >= start) & (slot < start + extra))
+            def _():
+                put(
+                    slot, slots + slot - start, 1 + turn_id,
+                    lambda other: {"col": donor, "row": other},
+                )
+
+        for first, last, count in own_cases(plan):
+            @pl.when((col >= first) & (col <= last) & (slot < count))
+            def _():
+                put(slot, slot, 0, lambda other: {"row": other})
+
+    def block(begin, count, line_row, home_row, piece):
+        home_at, _, width = spans(plan, home_row)[piece]
+        return home.at[:, pl.ds(begin, count), line_row, :, pl.ds(home_at, width)]
+
+    def settle(verb):
+        def one(begin, count, kind, step, piece, where, line_row, home_row):
+            at = block(begin, count, line_row, home_row, piece)
+            if kind == 0 and step == 0:
+                if verb == "send":
+                    pltpu.make_async_copy(at, at, send.at[0, 0, piece]).wait()
+                return
+            it = remote(at, at, kind, step, piece, where)
+            if verb == "send":
+                it.wait_send()
+            else:
+                it.wait_recv()
+
+        def all_of(begin, count, kind, where):
+            for step in range(rows):
+                if verb == "send":
+                    other = (row + step) % rows
+                    line_row, home_row = row, other
+                else:
+                    other = (row + rows - step) % rows
+                    line_row, home_row = other, row
+                each(
+                    home_row,
+                    lambda piece: one(
+                        begin, count, kind, step, piece, where(other), line_row, home_row
+                    ),
+                )
+
+        for first, last, count in own_cases(plan):
+            @pl.when((col >= first) & (col <= last))
+            def _():
+                all_of(0, count, 0, lambda other: {"row": other})
+
+        for donor, taker, turn_id in plan["moves"]:
+            mine, peer = (taker, donor) if verb == "send" else (donor, taker)
+
+            @pl.when(col == mine)
+            def _():
+                all_of(slots, extra, 1 + turn_id, lambda other: {"col": peer, "row": other})
+
+    @pl.loop(0, slots)
+    def _(i):
+        for n in range(2):
+            fetch(n, slot_of(i)).start()
+
+    @pl.loop(0, slots)
+    def _(i):
+        slot = slot_of(i)
+        for n in range(2):
+            fetch(n, slot).wait()
+        slot_out(plan, slot, held0, held1, turn, wh, wl, lines, scr, acc)
+
+        @pl.when(i > 0)
+        def _():
+            put_slot(slot_of(i + slots - 1))
+
+    put_slot(slot_of(slots - 1))
+    settle("recv")
+    settle("send")
+
+
+def lines_home(plan, got0, got1, turn, table):
+    slots, rows = plan["slots"], plan["rows"]
+    width = 2 * plan["low"] * LANES
+    devices = rows * plan["cols"]
+    dma = pltpu.SemaphoreType.DMA
+    held = pltpu.VMEM((slots, devices, 2, 2, SUBL, LANES), jnp.float32)
+    return pl.pallas_call(
+        functools.partial(lines_home_kernel, plan),
+        in_specs=[pl.BlockSpec(memory_space=pl.ANY)] * 2
+        + [pl.BlockSpec(memory_space=pltpu.VMEM)] * 3,
+        out_specs=pl.BlockSpec(memory_space=pl.ANY),
+        out_shape=jax.ShapeDtypeStruct(
+            (2, plan["groups"], rows, SUBL, plan["block_y"]), jnp.float32
+        ),
+        scratch_shapes=[
+            pltpu.VMEM((2 * HALF * SUBL, 2 * LANES), jnp.float32),
+            pltpu.VMEM((2 * plan["low"], 2, SUBL, LANES), jnp.float32),
+            held,
+            held,
+            pltpu.VMEM((slots, 2, SUBL, width), jnp.float32),
+            dma((2, slots)),
+            dma((3, rows, 2)),
+            dma((3, rows, 2)),
+        ],
+        compiler_params=pltpu.CompilerParams(has_side_effects=True, vmem_limit_bytes=60 << 20),
+        cost_estimate=pl.CostEstimate(flops=1 << 34, bytes_accessed=30 << 20, transcendentals=0),
+        name="lines_home",
+    )(got0, got1, turn, *table)
+
+
 def split_table(values):
     high = lax.reduce_precision(values, 8, 7)
     return high.astype(jnp.bfloat16), (values - high).astype(jnp.bfloat16)
@@ -829,8 +951,7 @@
     ]
     tables = column_tables(plan["length"])
     back = [across(columns(plan, part, tables)) for part in spread]
-    lines = lines_out(plan, *back, turn, lane_table(-1.0))
-    return exchange(plan, True, lines).reshape(field.shape)
+    return lines_home(plan, *back, turn, lane_table(-1.0)).reshape(field.shape)
 
 
 def fast_device(plan, start_field, section_field, start_term, first_term, second_term):

time: 751 us -> 741 us (0.987)
  Pallas kernels: 308 us -> 298 us
    pallas_call x2 -> x1, Pallas kernels: 158 us -> 66.9 us  [exchange(): pl.pallas_call(functools.partial(exchange_kernel, plan, back), in_specs=[...]
    pallas_call x1, Pallas kernels: 14.2 us -> 95.5 us  [lines_home(): pl.pallas_call(functools.partial(lines_home_kernel, plan), in_specs=[pl.B...]
where the time goes in v4:
time: 741 us; the launch traced here: 740 us
  waiting for transfers between devices  318 us (43%)
  Pallas kernels  298 us (40%)
  other arithmetic  70.9 us (10%)
  starting transfers between devices  52.6 us (7%)
    all_to_all x4, waiting for transfers between devices, across(): lax.all_to_all(lines, ('col', 'row'), split_axis=0, concat_axis=0, tiled=...  318 us
    pallas_call x2, Pallas kernels, columns(): pl.pallas_call(functools.partial(columns_kernel, plan), in_specs=[pl.Bloc...  114 us
    pallas_call x1, Pallas kernels, lines_home(): pl.pallas_call(functools.partial(lines_home_kernel, plan), in_specs=[pl.B...  95.5 us
    pallas_call x1, Pallas kernels, exchange(): pl.pallas_call(functools.partial(exchange_kernel, plan, back), in_specs=[...  66.9 us
    all_to_all x4, starting transfers between devices, across(): lax.all_to_all(lines, ('col', 'row'), split_axis=0, concat_axis=0, tiled=...  52.6 us
    sub x1, other arithmetic, section_weights(): weight_c = 4.0 * phi_three - phi_two  22.9 us
    pallas_call x2, Pallas kernels, lines_in(): pl.pallas_call(functools.partial(lines_in_kernel, plan, parity), grid=(sl...  21.3 us
    add x1, other arithmetic, fast_device(): damping * start_field + weight_a * start_term  21 us
  transfers between devices with their start and end apart: 4, of which 4 were waited for; matrix products, arithmetic and copies ran while one was open for 8% of the time, Pallas kernels for 17%

profile of v4, /device:TPU:9, one launch (start us, length us, event | category | flops | bytes accessed | tf_op | source)
XLA Modules:
  0.0 740.5 jit_solution(8548567245976899942)
XLA Ops:
  0.8 1.0 multiply_cosine_fusion
  1.9 0.6 slice_bitcast_fusion
  2.5 66.9 %home_lines.1.lines = f32[2,11,8,5632]{3,2,1,0:T(8,128)} custom-call(f32[2,16,4,8,2048]{4,3,2,1,0:T(8,128)} %bitcast.11), custom_call_target="tpu_custom_call" | custom-call | flops 17179869184 | bytes 16777216 | tf_op jit(solution)/shard_map/home_lines/pallas_call | solution.py:723
  69.5 0.8 fusion.94
  70.3 10.9 %lines_in.3 = f32[32,11,2,2,8,128]{5,4,3,2,1,0:T(8,128)} custom-call(f32[2,11,8,5632]{3,2,1,0:T(8,128)} %home_lines.1.lines, f32[32,2,128]{2,1,0:T(2,128)} %get-tuple-element.23.turn, bf16[256,256]{1,0:T(8,128)(2,1)} %get-tuple-element.21.wh, bf16[256,256]{1,0:T(8,128)(2,1)} %get-tuple-element.22.wl), custom_call_target="tpu_custom_call" | custom-call | flops 4294967296 | bytes 16777216 | tf_op jit(solution)/shard_map/lines_in/pallas_call | solution.py:438
  81.3 24.6 %all-to-all-start.2 = ((f32[32,11,2,2,8,128]{5,4,3,2,1,0:T(8,128)}), f32[32,11,2,2,8,128]{5,4,3,2,1,0:T(8,128)}, u32[]{:S(2)}, u32[]{:S(2)}) async-start(f32[32,11,2,2,8,128]{5,4,3,2,1,0:T(8,128)} %lines_in.3), calls=%async_computation.2 | async-start | bytes 11534336 | tf_op jit(solution)/shard_map/all_to_all | solution.py:943
  105.9 10.4 %lines_in.2 = f32[32,11,2,2,8,128]{5,4,3,2,1,0:T(8,128)} custom-call(f32[2,11,8,5632]{3,2,1,0:T(8,128)} %home_lines.1.lines, f32[32,2,128]{2,1,0:T(2,128)} %get-tuple-element.24.turn, bf16[256,256]{1,0:T(8,128)(2,1)} %get-tuple-element.21.wh, bf16[256,256]{1,0:T(8,128)(2,1)} %get-tuple-element.22.wl), custom_call_target="tpu_custom_call" | custom-call | flops 4294967296 | bytes 16777216 | tf_op jit(solution)/shard_map/lines_in/pallas_call | solution.py:438
  116.3 114.4 %all-to-all-done.2.src = f32[32,11,2,2,8,128]{5,4,3,2,1,0:T(8,128)} async-done(((f32[32,11,2,2,8,128]{5,4,3,2,1,0:T(8,128)}), f32[32,11,2,2,8,128]{5,4,3,2,1,0:T(8,128)}, u32[]{:S(2)}, u32[]{:S(2)}) %all-to-all-start.2) | async-done | bytes 5767200 | tf_op jit(solution)/shard_map/all_to_all | solution.py:943
  230.7 9.3 %all-to-all-start = ((f32[32,11,2,2,8,128]{5,4,3,2,1,0:T(8,128)}), f32[32,11,2,2,8,128]{5,4,3,2,1,0:T(8,128)}, u32[]{:S(2)}, u32[]{:S(2)}) async-start(f32[32,11,2,2,8,128]{5,4,3,2,1,0:T(8,128)} %lines_in.2), calls=%async_computation | async-start | bytes 11534336 | tf_op jit(solution)/shard_map/all_to_all | solution.py:943
  240.2 3.4 multiply_subtract_fusion
  243.7 4.4 fusion.1
  248.1 4.2 fusion
  252.2 57.1 %columns.3 = f32[32,11,2,2,8,128]{5,4,3,2,1,0:T(8,128)} custom-call(f32[32,11,2,2,8,128]{5,4,3,2,1,0:T(8,128)} %all-to-all-done.2.src, bf16[64,128,256]{2,1,0:T(8,128)(2,1)} %get-tuple-element.12.th, bf16[64,128,256]{2,1,0:T(8,128)(2,1)} %get-tuple-element.11.tl, bf16[64,256,128]{2,1,0:T(8,128)(2,1)} %get-tuple-element.10.fh, ...), custom_call_target="tpu_custom_call" | custom-call | flops 17179869184 | bytes 31457280 | tf_op jit(solution)/shard_map/columns/pallas_call | solution.py:524
  309.4 55.5 %all-to-all-done.src = f32[32,11,2,2,8,128]{5,4,3,2,1,0:T(8,128)} async-done(((f32[32,11,2,2,8,128]{5,4,3,2,1,0:T(8,128)}), f32[32,11,2,2,8,128]{5,4,3,2,1,0:T(8,128)}, u32[]{:S(2)}, u32[]{:S(2)}) %all-to-all-start) | async-done | bytes 5767200 | tf_op jit(solution)/shard_map/all_to_all | solution.py:943
  364.9 9.3 %all-to-all-start.3 = ((f32[32,11,2,2,8,128]{5,4,3,2,1,0:T(8,128)}), f32[32,11,2,2,8,128]{5,4,3,2,1,0:T(8,128)}, u32[]{:S(2)}, u32[]{:S(2)}) async-start(f32[32,11,2,2,8,128]{5,4,3,2,1,0:T(8,128)} %columns.3), calls=%async_computation.3 | async-start | bytes 11534336 | tf_op jit(solution)/shard_map/all_to_all | solution.py:943
  374.2 57.2 %columns.2 = f32[32,11,2,2,8,128]{5,4,3,2,1,0:T(8,128)} custom-call(f32[32,11,2,2,8,128]{5,4,3,2,1,0:T(8,128)} %all-to-all-done.src, bf16[64,128,256]{2,1,0:T(8,128)(2,1)} %get-tuple-element.12.th, bf16[64,128,256]{2,1,0:T(8,128)(2,1)} %get-tuple-element.11.tl, bf16[64,256,128]{2,1,0:T(8,128)(2,1)} %get-tuple-element.10.fh, ...), custom_call_target="tpu_custom_call" | custom-call | flops 17179869184 | bytes 31457280 | tf_op jit(solution)/shard_map/columns/pallas_call | solution.py:524
  431.4 67.7 %all-to-all-done.3.got1 = f32[32,11,2,2,8,128]{5,4,3,2,1,0:T(8,128)} async-done(((f32[32,11,2,2,8,128]{5,4,3,2,1,0:T(8,128)}), f32[32,11,2,2,8,128]{5,4,3,2,1,0:T(8,128)}, u32[]{:S(2)}, u32[]{:S(2)}) %all-to-all-start.3) | async-done | bytes 5767200 | tf_op jit(solution)/shard_map/all_to_all | solution.py:943
  499.1 9.4 %all-to-all-start.1 = ((f32[32,11,2,2,8,128]{5,4,3,2,1,0:T(8,128)}), f32[32,11,2,2,8,128]{5,4,3,2,1,0:T(8,128)}, u32[]{:S(2)}, u32[]{:S(2)}) async-start(f32[32,11,2,2,8,128]{5,4,3,2,1,0:T(8,128)} %columns.2), calls=%async_computation.1 | async-start | bytes 11534336 | tf_op jit(solution)/shard_map/all_to_all | solution.py:943
  508.5 22.9 %multiply_subtract_fusion.2 = (f32[512,2048]{1,0:T(8,128)}, f32[512,2048]{1,0:T(8,128)}, f32[512,2048]{1,0:T(8,128)}, f32[512,2048]{1,0:T(8,128)}) fusion(f32[512]{0:T(512)S(1)} %multiply_multiply_fusion.2, s32[2048]{0:T(1024)S(1)} %get-tuple-element.32, s32[2048]{0:T(1024)S(1)} %get-tuple-element.31, pred[2048]{0:T(1024)(128)(4,1)S(1)} %fusion.116, ...), kind=kLoop, calls=%fused_computation.110 | loop fusion | flops 102760448 | bytes 16799744 | tf_op jit(solution)/shard_map/sub | solution.py:46
  531.4 21.0 %multiply_add_fusion = f32[1,2,512,2048]{3,2,1,0:T(8,128)} fusion(f32[1,2,512,2048]{3,2,1,0:T(8,128)} %param.8, f32[1,2,512,2048]{3,2,1,0:T(8,128)} %param.9, f32[1,2,512,2048]{3,2,1,0:T(8,128)} %param.7, f32[1,2,512,2048]{3,2,1,0:T(8,128)} %param.5, f32[512,2048]{1,0:T(8,128)} %get-tuple-element.29, f32[512,2048]{1,0:T(8,128)} %get-tuple-element.28, ...), kind=kLoop, calls=%fused_computation.9 | loop fusion | flops 12582912 | bytes 54525952 | tf_op jit(solution)/shard_map/add | solution.py:966
  552.4 0.5 fusion.90
  552.9 80.4 %all-to-all-done.1.got0 = f32[32,11,2,2,8,128]{5,4,3,2,1,0:T(8,128)} async-done(((f32[32,11,2,2,8,128]{5,4,3,2,1,0:T(8,128)}), f32[32,11,2,2,8,128]{5,4,3,2,1,0:T(8,128)}, u32[]{:S(2)}, u32[]{:S(2)}) %all-to-all-start.1) | async-done | bytes 5767200 | tf_op jit(solution)/shard_map/all_to_all | solution.py:943
  633.3 95.5 %lines_home.1 = f32[2,16,4,8,2048]{4,3,2,1,0:T(8,128)} custom-call(f32[32,11,2,2,8,128]{5,4,3,2,1,0:T(8,128)} %all-to-all-done.1.got0, f32[32,11,2,2,8,128]{5,4,3,2,1,0:T(8,128)} %all-to-all-done.3.got1, f32[2,32,2,128]{3,2,1,0:T(2,128)} %copy-done, bf16[256,256]{1,0:T(8,128)(2,1)} %get-tuple-element.14.wh, bf16[256,256]{1,0:T(8,128)(2,1)} %get-tuple-element.13.wl), custom_call_target="tpu_custom_call" | custom-call | flops 17179869184 | bytes 31457280 | tf_op jit(solution)/shard_map/lines_home/pallas_call | solution.py:868
  728.8 11.6 %select_add_fusion = f32[1,2,512,2048]{3,2,1,0:T(8,128)} fusion(f32[1,2,512,2048]{3,2,1,0:T(8,128)} %multiply_add_fusion, f32[1,2,512,2048]{3,2,1,0:T(8,128)} %bitcast.9, f32[512,2048]{1,0:T(8,128)} %get-tuple-element.8, pred[512,2048]{1,0:T(8,128)(4,1)S(1)} %fusion.90), kind=kLoop, calls=%fused_computation.8 | loop fusion | flops 6291456 | bytes 30408704 | tf_op jit(solution)/shard_map/add | solution.py:973
  (13 shorter events, 1.1 us)
Async XLA Ops:
  1.9 67.6 %copy-start = (f32[2,32,2,128]{3,2,1,0:T(2,128)}, f32[2,32,2,128]{3,2,1,0:T(2,128)S(1)}, u32[]{:S(2)}) copy-start(f32[2,32,2,128]{3,2,1,0:T(2,128)S(1)} %maximum_bitcast_fusion.turn) | copy-start | bytes 196612
  81.3 149.4 %all-to-all-start.2 = ((f32[32,11,2,2,8,128]{5,4,3,2,1,0:T(8,128)}), f32[32,11,2,2,8,128]{5,4,3,2,1,0:T(8,128)}, u32[]{:S(2)}, u32[]{:S(2)}) async-start(f32[32,11,2,2,8,128]{5,4,3,2,1,0:T(8,128)} %lines_in.3), calls=%async_computation.2 | async-start | bytes 11534336 | tf_op jit(solution)/shard_map/all_to_all | solution.py:943
  230.7 134.2 %all-to-all-start = ((f32[32,11,2,2,8,128]{5,4,3,2,1,0:T(8,128)}), f32[32,11,2,2,8,128]{5,4,3,2,1,0:T(8,128)}, u32[]{:S(2)}, u32[]{:S(2)}) async-start(f32[32,11,2,2,8,128]{5,4,3,2,1,0:T(8,128)} %lines_in.2), calls=%async_computation | async-start | bytes 11534336 | tf_op jit(solution)/shard_map/all_to_all | solution.py:943
  364.9 134.2 %all-to-all-start.3 = ((f32[32,11,2,2,8,128]{5,4,3,2,1,0:T(8,128)}), f32[32,11,2,2,8,128]{5,4,3,2,1,0:T(8,128)}, u32[]{:S(2)}, u32[]{:S(2)}) async-start(f32[32,11,2,2,8,128]{5,4,3,2,1,0:T(8,128)} %columns.3), calls=%async_computation.3 | async-start | bytes 11534336 | tf_op jit(solution)/shard_map/all_to_all | solution.py:943
  499.1 134.2 %all-to-all-start.1 = ((f32[32,11,2,2,8,128]{5,4,3,2,1,0:T(8,128)}), f32[32,11,2,2,8,128]{5,4,3,2,1,0:T(8,128)}, u32[]{:S(2)}, u32[]{:S(2)}) async-start(f32[32,11,2,2,8,128]{5,4,3,2,1,0:T(8,128)} %columns.2), calls=%async_computation.1 | async-start | bytes 11534336 | tf_op jit(solution)/shard_map/all_to_all | solution.py:943
